TPU v7x, 256 devices: a whole 4x4x8 slice. The times are simulated.
256 devices in a mesh: grp: 8 (over z), sp: 32 (over y, x, core).
Axes of the slice: x: 4, y: 4, z: 8, core: 2. Of those that a mesh axis runs over, the one named last changes fastest.
Arguments:
- tokens: bfloat16 [16384, 2880], P(('grp', 'sp')), may hold values from -36 to 36
- query_weight: bfloat16 [2880, 2048], P(None, 'sp'), may hold values from -0.109375 to 0.109375
- key_value_weight: bfloat16 [2880, 1024], replicated, may hold values from -0.109375 to 0.109375
- block_places: int32 [32], replicated, may hold values from 0 to 31, each once
- sinks: float32 [32], replicated, may hold values from -1 to 5
Outputs:
- attended: bfloat16 [16384, 2048], P(('grp', 'sp'))
Inputs may be any that keep to these rules, and one draw needn't show every extreme that they name: `block_places`: every sequence block appears once.
All inputs are finite; a program needn't handle non-finite values.
Results may differ from a plain program's by a relative error of at most 0.008.
The roundings to bfloat16 on the way count: a program that leaves them out, or rounds other values in their place, can miss the bound.
Values may be sent and summed in bfloat16 or wider, within the bound.
No kernel may reach another device: no remote copies, remote signals or barrier semaphores. Data moves between devices by JAX's collectives and lax.ppermute only.
A program may use at most 128 MiB of HBM per device.

v0:
```python
import jax
import jax.numpy as jnp
from jax import lax
from jax.experimental import pallas as pl
from jax.experimental.pallas import tpu as pltpu
from jax.sharding import Mesh, PartitionSpec as P


HEAD = 64
NBLK = 32
BLK = 512
ROWS = 64
ROPE_BASE = 150000.0
NEG = -1e30
EXPC = 1.4426950408889634 / 8.0
BF = jnp.bfloat16
F32 = jnp.float32


def attend_kernel(
    inv_ref, meta_ref, sink_ref, own_ref, other_ref, q_ref, o_ref, kvs, vts, qs, s_scr, cm_scr
):
    off = meta_ref[0]
    y_tile = meta_ref[1]
    core = meta_ref[2]

    @pl.loop(0, NBLK)
    def _(s):
        b = inv_ref[s]
        for px in range(4):
            for ref, at in ((own_ref, core), (other_ref, 1 - core)):
                start = pl.multiple_of(s * BLK + (2 * px + at) * ROWS, ROWS)
                kvs[pl.ds(start, ROWS), :] = ref[lax.rem(b, 4), px, b // 4]
        t = jnp.transpose(kvs[pl.ds(pl.multiple_of(s * BLK, BLK), BLK), :])
        vts[s, 0:HEAD, :] = t[HEAD : 2 * HEAD, :]
        vts[s, HEAD : HEAD + 16, :] = jnp.ones((16, BLK), BF)

    for k in range(8):
        rows = jnp.transpose(q_ref[k])
        wide = jnp.concatenate([rows, jnp.zeros((4 * ROWS, HEAD), BF)], axis=1)
        qs[k] = wide.reshape(4, ROWS, 2 * HEAD)

    def qtile(i):
        parts = []
        for j in range(4):
            b = inv_ref[i * 4 + j]
            parts.append(qs[b // 4, lax.rem(lax.rem(b, 4) - y_tile + 4, 4)])
        return jnp.concatenate(parts, axis=0)

    def qk(i, s, slot, diag):
        keys = kvs[pl.ds(pl.multiple_of(s * BLK, BLK), BLK), :]
        scores = lax.dot_general(
            keys, qtile(i), (((1,), (1,)), ((), ())), preferred_element_type=F32
        )
        if diag is not None:
            row = lax.broadcasted_iota(jnp.int32, (BLK, 256), 0) + diag * BLK
            col = lax.broadcasted_iota(jnp.int32, (1, 256), 1)
            limit = (col // ROWS) * BLK + lax.rem(col, ROWS) + off
            scores = jnp.where(row <= limit, scores, NEG)
        s_scr[slot] = scores
        cm_scr[slot] = jnp.max(scores.reshape(BLK // 8, 8, 256), axis=0)

    def soft(s, slot, m, acc):
        new = jnp.maximum(m, jnp.max(cm_scr[slot], axis=0, keepdims=True))
        factor = jnp.exp2((m - new) * EXPC)
        weight = jnp.exp2((s_scr[slot] - new) * EXPC).astype(BF)
        return new, acc * factor + jnp.dot(vts[s], weight, preferred_element_type=F32)

    def tile(i, _):
        m = jnp.full((1, 256), sink_ref[0] * 8.0, F32)
        acc = jnp.concatenate([jnp.zeros((HEAD, 256), F32), jnp.ones((16, 256), F32)], axis=0)

        def full(j, carry):
            m, acc = carry
            for u in range(4):
                if u < 3:
                    qk(i, j * 4 + u + 1, (u + 1) % 2, None)
                else:

                    @pl.when(j + 1 < i)
                    def _():
                        qk(i, j * 4 + 4, 0, None)

                    @pl.when(j + 1 == i)
                    def _():
                        qk(i, j * 4 + 4, 0, 0)

                m, acc = soft(j * 4 + u, u % 2, m, acc)
            return m, acc

        m, acc = lax.fori_loop(0, i, full, (m, acc))
        for u in range(4):
            if u < 3:
                qk(i, i * 4 + u + 1, (u + 1) % 2, u + 1)
            else:
                qk(jnp.minimum(i + 1, 7), 0, 0, None)
            m, acc = soft(i * 4 + u, u % 2, m, acc)
        done = jnp.transpose(acc[0:HEAD] / acc[HEAD : HEAD + 1]).astype(BF)
        for j in range(4):
            rows = done[j * ROWS : (j + 1) * ROWS]
            o_ref[inv_ref[i * 4 + j]] = jnp.concatenate([rows[0:32], rows[32:64]], axis=1)
        return 0

    qk(0, 0, 0, 0)
    lax.fori_loop(0, 8, tile, 0)


def attend(inv, meta, sink, own, other, q):
    return pl.pallas_call(
        attend_kernel,
        out_shape=jax.ShapeDtypeStruct((NBLK, 32, 128), BF),
        in_specs=[pl.BlockSpec(memory_space=pltpu.SMEM)] * 3
        + [pl.BlockSpec(memory_space=pltpu.VMEM)] * 3,
        out_specs=pl.BlockSpec(memory_space=pltpu.VMEM),
        scratch_shapes=[
            pltpu.VMEM((NBLK * BLK, 2 * HEAD), BF),
            pltpu.VMEM((NBLK, HEAD + 16, BLK), BF),
            pltpu.VMEM((8, 4, ROWS, 2 * HEAD), BF),
            pltpu.VMEM((2, BLK, 256), F32),
            pltpu.VMEM((2, 8, 256), F32),
        ],
        compiler_params=pltpu.CompilerParams(vmem_limit_bytes=50 * 2**20),
        name="attend",
    )(inv, meta, sink, own, other, q)


def pull(value, axis, shift):
    size = lax.axis_size(axis)
    return lax.ppermute(value, axis, [((i + shift) % size, i) for i in range(size)])


def swap(value):
    return lax.ppermute(value, "c", [(0, 1), (1, 0)])


def ordered(own, other, c):
    return lax.dynamic_slice_in_dim(jnp.stack([own, other, own]), c, 2, 0)


def rotations(places):
    inverse = ROPE_BASE ** (-(jnp.arange(HEAD // 2, dtype=F32) * 2.0) / HEAD)
    angles = places.astype(F32)[None, :] * inverse[:, None]
    return jnp.cos(angles), jnp.sin(angles)


def per_device(tokens, query_weight, key_value_weight, block_places, sinks):
    z, y, x, c = (lax.axis_index(a) for a in "zyxc")
    weight_rows = query_weight.T
    row_pieces = [tokens] + [pull(tokens, "y", s) for s in (1, 2, 3)]
    weight_pieces = [weight_rows] + [pull(weight_rows, "x", s) for s in (1, 2, 3)]

    table = jnp.arange(NBLK, dtype=jnp.int32)
    block_of = jnp.sum(
        jnp.where(block_places[None, :] == table[:, None], table[None, :], 0), axis=1
    ).astype(jnp.int32)
    own_blocks = 4 * z + (y + jnp.arange(4, dtype=jnp.int32)) % 4
    own_places = jnp.sum(
        jnp.where(own_blocks[:, None] == table[None, :], block_places[None, :], 0), axis=1
    )
    places = (
        own_places[:, None] * BLK + (2 * x + c) * ROWS + jnp.arange(ROWS, dtype=jnp.int32)[None, :]
    )

    cos, sin = (t.T[:, None, :] for t in rotations(places[0]))
    kv = jnp.dot(tokens, key_value_weight, preferred_element_type=F32)
    keys = kv[:, :512].reshape(ROWS, 8, 2, 32)
    first, second = keys[:, :, 0], keys[:, :, 1]
    keys = jnp.concatenate([first * cos - second * sin, second * cos + first * sin], axis=-1)
    pair = jnp.concatenate([keys, kv[:, 512:].reshape(ROWS, 8, HEAD)], axis=-1).astype(BF)
    pair = lax.all_to_all(jnp.transpose(pair, (1, 0, 2)), "z", 0, 0, tiled=True)
    copies = jnp.broadcast_to(pair[None], (16, 8, ROWS, 2 * HEAD)).reshape(128, ROWS, 2 * HEAD)
    own = lax.all_to_all(copies, ("y", "x"), 0, 0, tiled=True)
    own = own.reshape(4, 4, 8, ROWS, 2 * HEAD)
    other = swap(own)

    rows = jnp.concatenate(row_pieces, axis=0)
    weights = jnp.concatenate(weight_pieces, axis=0)
    weights_other = swap(weights)
    cos_q, sin_q = rotations(places.reshape(4 * ROWS))

    def project(w):
        q = lax.dot_general(w, rows, (((1,), (1,)), ((), ())), preferred_element_type=F32)
        q = q.reshape(4, 2, 32, 4 * ROWS)
        a, b = q[:, 0], q[:, 1]
        return jnp.concatenate([a * cos_q - b * sin_q, b * cos_q + a * sin_q], axis=1).astype(BF)

    q = ordered(project(weights), project(weights_other), c)
    q = lax.dynamic_slice_in_dim(jnp.concatenate([q, q], axis=1), (4 - x) % 4, 4, 1)
    q = jnp.transpose(q.reshape(2, 2, 2, HEAD, 4 * ROWS), (2, 0, 1, 3, 4))
    q = lax.all_to_all(q.reshape(8, HEAD, 4 * ROWS), "y", 0, 0, tiled=True)
    q = lax.all_to_all(q, "z", 0, 0, tiled=True)

    slot = jnp.arange(3, dtype=jnp.int32)
    meta = jnp.where(slot == 0, ROWS * (2 * x + c), jnp.where(slot == 1, z // 2, c))
    sink = lax.dynamic_slice_in_dim(sinks, 4 * z + y, 1, 0)
    out = attend(block_of, meta.astype(jnp.int32), sink, own, other, q)

    out = lax.all_to_all(out, ("z", "y"), 0, 0, tiled=True)
    out = out.reshape(32, 32, 2, HEAD)
    return jnp.transpose(out, (2, 1, 0, 3)).reshape(ROWS, 32 * HEAD)


def solution(mesh):
    fine = Mesh(mesh.devices.reshape(8, 4, 4, 2), ("z", "y", "x", "c"))
    whole = ("z", "y", "x", "c")

    return jax.shard_map(
        per_device,
        mesh=fine,
        in_specs=(P(whole, None), P(None, ("y", "x", "c")), P(), P(), P()),
        out_specs=P(whole, None),
        check_vma=False,
    )
```

profile of v0, /device:TPU:2, one launch (start us, length us, event | category | flops | bytes accessed | tf_op | source)
XLA Modules:
  0.0 176.8 jit_solution(10383172861785260033)
XLA Ops:
  0.0 0.0 copy-start.4
  0.0 4.0 %fusion.13 = f32[64,1024]{1,0:T(8,128)S(1)} fusion(bf16[64,2880]{1,0:T(8,128)(2,1)} %param.5, bf16[2880,1024]{1,0:T(8,128)(2,1)} %param.7), kind=kOutput, calls=%fused_computation.57 | convolution fusion | flops 377487360 | bytes 6529024 | tf_op jit(solution)/shard_map/dot_general | solution.py:165
  4.1 0.2 select_reduce_fusion.1
  4.3 0.1 fusion.12
  4.3 0.1 copy.48
  4.5 0.1 multiply_cosine_fusion.1
  4.7 0.1 copy.50
  4.8 0.1 copy.51
  4.9 0.1 reshape.272
  5.1 0.1 maximum_bitcast_fusion
  5.2 17.4 %all_to_all.25 = bf16[8,64,128]{2,1,0:T(8,128)(2,1)S(1)} all-to-all(bf16[8,64,128]{2,1,0:T(8,128)(2,1)S(1)} %maximum_bitcast_fusion), channel_id=1, replica_groups=mesh['z'=8,'y'=4,'x'=4,'c'=2] {'z'}, dimensions={0} | all-to-all | bytes 262144 | tf_op jit(solution)/shard_map/all_to_all | solution.py:170
  22.6 1.9 %broadcast_in_dim.42 = bf16[16,8,64,128]{3,2,1,0:T(8,128)(2,1)} broadcast(bf16[8,64,128]{2,1,0:T(8,128)(2,1)S(1)} %all_to_all.25), dimensions={1,2,3} | broadcast | bytes 2228224 | tf_op jit(solution)/shard_map/broadcast_in_dim | solution.py:171
  24.5 7.6 %all-to-all-start.1 = ((bf16[128,64,128]{2,1,0:T(8,128)(2,1)}), bf16[128,64,128]{2,1,0:T(8,128)(2,1)S(1)}, u32[]{:S(2)}, u32[]{:S(2)}) async-start(bf16[128,64,128]{2,1,0:T(8,128)(2,1)} %bitcast.95), calls=%async_computation.1 | async-start | bytes 4194304 | tf_op jit(solution)/shard_map/all_to_all | solution.py:172
  32.1 0.2 collective-permute-start.1
  32.3 2.7 %collective-permute-start.2 = (bf16[64,2880]{1,0:T(8,128)(2,1)}, bf16[64,2880]{1,0:T(8,128)(2,1)}, u32[]{:S(2)}, u32[]{:S(2)}) collective-permute-start(bf16[64,2880]{1,0:T(8,128)(2,1)} %bitcast.7), channel_id=1, source_target_pairs={{4,0},{6,2},{0,4},{2,6},{5,1},{7,3},{1,5},{3,7},{12,8},{14,10},{8,... | collective-permute-start | bytes 1105928 | tf_op jit(solution)/shard_map/ppermute | solution.py:129
  35.0 1.8 %collective-permute-start.3 = (bf16[64,2880]{1,0:T(8,128)(2,1)}, bf16[64,2880]{1,0:T(8,128)(2,1)}, u32[]{:S(2)}, u32[]{:S(2)}) collective-permute-start(bf16[64,2880]{1,0:T(8,128)(2,1)} %bitcast.7), channel_id=1, source_target_pairs={{6,0},{0,2},{2,4},{4,6},{7,1},{1,3},{3,5},{5,7},{14,8},{8,10},{10,... | collective-permute-start | bytes 1105928 | tf_op jit(solution)/shard_map/ppermute | solution.py:129
  36.8 2.7 %collective-permute-start.4 = (bf16[64,2880]{1,0:T(8,128)(2,1)S(1)}, bf16[64,2880]{1,0:T(8,128)(2,1)}, u32[]{:S(2)}, u32[]{:S(2)}) collective-permute-start(bf16[64,2880]{1,0:T(8,128)(2,1)S(1)} %copy-done.2), channel_id=1, source_target_pairs={{8,0},{16,8},{24,16},{0,24},{9,1},{17,9},{25,17},{1,25},{10,2},{18... | collective-permute-start | bytes 1105928 | tf_op jit(solution)/shard_map/ppermute | solution.py:129
  39.5 0.9 collective-permute-start.5
  40.3 0.1 convert_element_type.33
  40.4 0.8 constant_dynamic-update-slice_fusion.3
  41.2 31.6 %collective-permute-done.1 = bf16[64,2880]{1,0:T(8,128)(2,1)} collective-permute-done((bf16[64,2880]{1,0:T(8,128)(2,1)}, bf16[64,2880]{1,0:T(8,128)(2,1)}, u32[]{:S(2)}, u32[]{:S(2)}) %collective-permute-start.1) | collective-permute-done | bytes 368672 | tf_op jit(solution)/shard_map/ppermute | solution.py:129
  72.7 1.5 collective-permute-start.6
  74.3 0.0 collective-permute-done.2
  74.3 0.0 collective-permute-done.3
  74.3 2.6 %pad_maximum_fusion = bf16[256,2880]{1,0:T(8,128)(2,1)} fusion(bf16[64,2880]{1,0:T(8,128)(2,1)} %collective-permute-done.3, bf16[64,2880]{1,0:T(8,128)(2,1)} %collective-permute-done.2, bf16[64,2880]{1,0:T(8,128)(2,1)} %collective-permute-done.1, bf16[64,2880]{1,0:T(8,128)(2,1)} %bitcast.7), kind=kLoop, calls=%fused_computation | loop fusion | flops 5898240 | bytes 2949120 | tf_op jit(solution)/shard_map/concatenate | solution.py:177
  76.9 2.6 %copy.55 = bf16[256,2880]{0,1:T(8,128)(2,1)} copy(bf16[256,2880]{1,0:T(8,128)(2,1)} %pad_maximum_fusion) | data formatting | bytes 2949120 | tf_op jit(solution)/shard_map/concatenate | solution.py:177
  79.5 0.2 multiply_cosine_fusion
  79.7 1.7 constant_dynamic-update-slice_fusion.2
  81.5 0.5 collective-permute-start
  82.0 0.8 constant_dynamic-update-slice_fusion.1
  82.8 0.9 collective-permute-done.6
  83.7 0.8 constant_dynamic-update-slice_fusion
  84.5 2.1 %fusion.14 = f32[256,256]{1,0:T(8,128)S(1)} fusion(bf16[256,2880]{1,0:T(8,128)(2,1)S(1)} %copy-done, bf16[256,2880]{1,0:T(8,128)(2,1)} %constant_dynamic-update-slice_fusion), kind=kOutput, calls=%fused_computation.58 | convolution fusion | flops 377487360 | bytes 3211264 | tf_op jit(solution)/shard_map/dot_general | solution.py:182
  86.6 2.0 %fusion.15 = f32[256,256]{1,0:T(8,128)S(1)} fusion(bf16[256,2880]{0,1:T(8,128)(2,1)} %collective-permute-done.7, bf16[256,2880]{1,0:T(8,128)(2,1)S(1)} %copy-done.1), kind=kOutput, calls=%fused_computation.59 | convolution fusion | flops 377487360 | bytes 3211264 | tf_op jit(solution)/shard_map/dot_general | solution.py:182
  88.6 0.1 fusion.9
  88.7 0.0 copy-start.3
  88.7 0.2 fusion.2
  88.9 0.1 fusion.5
  89.1 9.7 %all_to_all.26 = bf16[8,64,256]{2,1,0:T(8,128)(2,1)} all-to-all(bf16[8,64,256]{2,1,0:T(8,128)(2,1)S(1)} %bitcast.101), channel_id=1, replica_groups=mesh['z'=8,'y'=4,'x'=4,'c'=2] {'y'}, dimensions={0} | all-to-all | bytes 524288 | tf_op jit(solution)/shard_map/all_to_all | solution.py:190
  98.8 3.6 %all-to-all-start.3 = ((bf16[8,64,256]{2,1,0:T(8,128)(2,1)}), bf16[8,64,256]{2,1,0:T(8,128)(2,1)S(1)}, u32[]{:S(2)}, u32[]{:S(2)}) async-start(bf16[8,64,256]{2,1,0:T(8,128)(2,1)} %all_to_all.26), calls=%async_computation.3 | async-start | bytes 524288 | tf_op jit(solution)/shard_map/all_to_all | solution.py:191
  102.4 0.6 dynamic_slice.9.sink_ref
  103.0 0.1 select_reduce_fusion.inv_ref
  103.1 9.6 %all-to-all-done.3.q_ref = bf16[8,64,256]{2,1,0:T(8,128)(2,1)S(1)} async-done(((bf16[8,64,256]{2,1,0:T(8,128)(2,1)}), bf16[8,64,256]{2,1,0:T(8,128)(2,1)S(1)}, u32[]{:S(2)}, u32[]{:S(2)}) %all-to-all-start.3) | async-done | bytes 262176 | tf_op jit(solution)/shard_map/all_to_all | solution.py:191
  112.8 47.4 %attend.1 = bf16[32,32,128]{2,1,0:T(8,128)(2,1)S(1)} custom-call(s32[32]{0:T(128)S(1)} %select_reduce_fusion.inv_ref, s32[3]{0:T(128)S(1)} %compare_select_fusion.3.meta_ref, f32[1]{0:T(128)} %dynamic_slice.9.sink_ref, bf16[4,4,8,64,128]{4,3,2,1,0:T(8,128)(2,1)S(1)} %bitcast.94, bf16[4,4,8,64,128]{4,3,2,1,0:T(8,128)(2,1)} %collective-permute-done.other_ref, ...), custom_call_target="tpu_custom_call" | custom-call | tf_op jit(solution)/shard_map/attend/pallas_call | solution.py:109
  160.1 14.9 %all_to_all.27 = bf16[32,32,128]{2,1,0:T(8,128)(2,1)S(1)} all-to-all(bf16[32,32,128]{2,1,0:T(8,128)(2,1)S(1)} %attend.1), channel_id=1, replica_groups=mesh['z'=8,'y'=4,'x'=4,'c'=2] {'z','y'}, dimensions={0} | all-to-all | bytes 524288 | tf_op jit(solution)/shard_map/all_to_all | solution.py:198
  175.1 0.2 reshape.279
  175.3 0.3 copy.59
  175.7 1.2 reshape.280
  (24 shorter events, 0.2 us)
Async XLA Ops:
  0.0 4.1 %copy-start.4 = (s32[32]{0:T(128)S(1)}, s32[32]{0:T(128)}, u32[]{:S(2)}) copy-start(s32[32]{0:T(128)} %param.8) | copy-start | bytes 388
  24.5 12.3 %copy-start.2 = (bf16[64,2880]{1,0:T(8,128)(2,1)S(1)}, bf16[64,2880]{1,0:T(8,128)(2,1)}, u32[]{:S(2)}) copy-start(bf16[64,2880]{1,0:T(8,128)(2,1)} %param.5) | copy-start | bytes 1105924
  24.5 57.0 %all-to-all-start.1 = ((bf16[128,64,128]{2,1,0:T(8,128)(2,1)}), bf16[128,64,128]{2,1,0:T(8,128)(2,1)S(1)}, u32[]{:S(2)}, u32[]{:S(2)}) async-start(bf16[128,64,128]{2,1,0:T(8,128)(2,1)} %bitcast.95), calls=%async_computation.1 | async-start | bytes 4194304 | tf_op jit(solution)/shard_map/all_to_all | solution.py:172
  32.1 40.7 %collective-permute-start.1 = (bf16[64,2880]{1,0:T(8,128)(2,1)}, bf16[64,2880]{1,0:T(8,128)(2,1)}, u32[]{:S(2)}, u32[]{:S(2)}) collective-permute-start(bf16[64,2880]{1,0:T(8,128)(2,1)} %bitcast.7), channel_id=1, source_target_pairs={{2,0},{4,2},{6,4},{0,6},{3,1},{5,3},{7,5},{1,7},{10,8},{12,10},{14... | collective-permute-start | bytes 1105928 | tf_op jit(solution)/shard_map/ppermute | solution.py:129
  32.3 42.0 %collective-permute-start.2 = (bf16[64,2880]{1,0:T(8,128)(2,1)}, bf16[64,2880]{1,0:T(8,128)(2,1)}, u32[]{:S(2)}, u32[]{:S(2)}) collective-permute-start(bf16[64,2880]{1,0:T(8,128)(2,1)} %bitcast.7), channel_id=1, source_target_pairs={{4,0},{6,2},{0,4},{2,6},{5,1},{7,3},{1,5},{3,7},{12,8},{14,10},{8,... | collective-permute-start | bytes 1105928 | tf_op jit(solution)/shard_map/ppermute | solution.py:129
  35.0 39.3 %collective-permute-start.3 = (bf16[64,2880]{1,0:T(8,128)(2,1)}, bf16[64,2880]{1,0:T(8,128)(2,1)}, u32[]{:S(2)}, u32[]{:S(2)}) collective-permute-start(bf16[64,2880]{1,0:T(8,128)(2,1)} %bitcast.7), channel_id=1, source_target_pairs={{6,0},{0,2},{2,4},{4,6},{7,1},{1,3},{3,5},{5,7},{14,8},{8,10},{10,... | collective-permute-start | bytes 1105928 | tf_op jit(solution)/shard_map/ppermute | solution.py:129
  36.8 42.9 %collective-permute-start.4 = (bf16[64,2880]{1,0:T(8,128)(2,1)S(1)}, bf16[64,2880]{1,0:T(8,128)(2,1)}, u32[]{:S(2)}, u32[]{:S(2)}) collective-permute-start(bf16[64,2880]{1,0:T(8,128)(2,1)S(1)} %copy-done.2), channel_id=1, source_target_pairs={{8,0},{16,8},{24,16},{0,24},{9,1},{17,9},{25,17},{1,25},{10,2},{18... | collective-permute-start | bytes 1105928 | tf_op jit(solution)/shard_map/ppermute | solution.py:129
  39.5 42.5 %collective-permute-start.5 = (bf16[64,2880]{1,0:T(8,128)(2,1)S(1)}, bf16[64,2880]{1,0:T(8,128)(2,1)S(1)}, u32[]{:S(2)}, u32[]{:S(2)}) collective-permute-start(bf16[64,2880]{1,0:T(8,128)(2,1)S(1)} %copy-done.2), channel_id=1, source_target_pairs={{16,0},{24,8},{0,16},{8,24},{17,1},{25,9},{1,17},{9,25},{18,2},{26... | collective-permute-start | bytes 1105928 | tf_op jit(solution)/shard_map/ppermute | solution.py:129
  72.7 11.0 %collective-permute-start.6 = (bf16[64,2880]{1,0:T(8,128)(2,1)S(1)}, bf16[64,2880]{1,0:T(8,128)(2,1)S(1)}, u32[]{:S(2)}, u32[]{:S(2)}) collective-permute-start(bf16[64,2880]{1,0:T(8,128)(2,1)S(1)} %copy-done.2), channel_id=1, source_target_pairs={{24,0},{0,8},{8,16},{16,24},{25,1},{1,9},{9,17},{17,25},{26,2},{2,... | collective-permute-start | bytes 1105928 | tf_op jit(solution)/shard_map/ppermute | solution.py:129
  79.5 7.1 %collective-permute-start.7 = (bf16[256,2880]{0,1:T(8,128)(2,1)}, bf16[256,2880]{0,1:T(8,128)(2,1)}, u32[]{:S(2)}, u32[]{:S(2)}) collective-permute-start(bf16[256,2880]{0,1:T(8,128)(2,1)} %copy.55), channel_id=1, source_target_pairs={{0,1},{1,0},{2,3},{3,2},{4,5},{5,4},{6,7},{7,6},{8,9},{9,8},{10,11... | collective-permute-start | bytes 4423688 | tf_op jit(solution)/shard_map/ppermute | solution.py:133
  81.5 3.0 %copy-start = (bf16[256,2880]{1,0:T(8,128)(2,1)S(1)}, bf16[256,2880]{1,0:T(8,128)(2,1)}, u32[]{:S(2)}) copy-start(bf16[256,2880]{1,0:T(8,128)(2,1)} %pad_maximum_fusion) | copy-start | bytes 4423684
  81.5 31.3 %collective-permute-start = (bf16[4,4,8,64,128]{4,3,2,1,0:T(8,128)(2,1)S(1)}, bf16[4,4,8,64,128]{4,3,2,1,0:T(8,128)(2,1)}, u32[]{:S(2)}, u32[]{:S(2)}) collective-permute-start(bf16[4,4,8,64,128]{4,3,2,1,0:T(8,128)(2,1)S(1)} %bitcast.93), channel_id=1, source_target_pairs={{0,1},{1,0},{2,3},{3,2},{4,5},{5,4},{6,7},{7,6},{8,9},{9,8},{10,11... | collective-permute-start | bytes 6291464 | tf_op jit(solution)/shard_map/ppermute | solution.py:133
  84.5 2.1 %copy-start.1 = (bf16[256,2880]{1,0:T(8,128)(2,1)S(1)}, bf16[256,2880]{1,0:T(8,128)(2,1)}, u32[]{:S(2)}) copy-start(bf16[256,2880]{1,0:T(8,128)(2,1)} %constant_dynamic-update-slice_fusion) | copy-start | bytes 4423684
  88.7 13.7 %copy-start.3 = (f32[32]{0:T(128)S(1)}, f32[32]{0:T(128)}, u32[]{:S(2)}) copy-start(f32[32]{0:T(128)} %param.9) | copy-start | bytes 388
  98.8 14.0 %all-to-all-start.3 = ((bf16[8,64,256]{2,1,0:T(8,128)(2,1)}), bf16[8,64,256]{2,1,0:T(8,128)(2,1)S(1)}, u32[]{:S(2)}, u32[]{:S(2)}) async-start(bf16[8,64,256]{2,1,0:T(8,128)(2,1)} %all_to_all.26), calls=%async_computation.3 | async-start | bytes 524288 | tf_op jit(solution)/shard_map/all_to_all | solution.py:191
where the time goes:
time: 177 us
  Pallas kernels  47.4 us (27%)
  waiting for transfers between devices  42.2 us (24%)
  blocking collectives  42 us (24%)
  starting transfers between devices  21.5 us (12%)
  local copies, waits for them, and re-layouts  11.5 us (6%)
  matrix products  8.1 us (5%)
  other arithmetic  3.89 us (2%)
    pallas_call x1, Pallas kernels, attend(): pl.pallas_call(attend_kernel, out_shape=jax.ShapeDtypeStruct((NBLK, 32, 1...  47.4 us
    ppermute x6, waiting for transfers between devices, pull(): lax.ppermute(value, axis, [((i + shift) % size, i) for i in range(size)])  32.5 us
    all_to_all x1, blocking collectives, per_device(): pair = lax.all_to_all(jnp.transpose(pair, (1, 0, 2)), 'z', 0, 0, tiled=True)  17.4 us
    all_to_all x1, blocking collectives, per_device(): out = lax.all_to_all(out, ('z', 'y'), 0, 0, tiled=True)  14.9 us
    ppermute x6, starting transfers between devices, pull(): lax.ppermute(value, axis, [((i + shift) % size, i) for i in range(size)])  9.77 us
    all_to_all x1, blocking collectives, per_device(): q = lax.all_to_all(q.reshape(8, HEAD, 4 * ROWS), 'y', 0, 0, tiled=True)  9.73 us
    all_to_all x1, waiting for transfers between devices, per_device(): q = lax.all_to_all(q, 'z', 0, 0, tiled=True)  9.65 us
    all_to_all x1, starting transfers between devices, per_device(): own = lax.all_to_all(copies, ('y', 'x'), 0, 0, tiled=True)  7.61 us
  transfers between devices with their start and end apart: 10, of which 3 were waited for; matrix products, arithmetic and copies ran while one was open for 8% of the time, Pallas kernels for 0%

commit v1 on v0

--- a/solution.py
+++ b/solution.py
@@ -18,19 +18,21 @@
 
 
 def attend_kernel(
-    inv_ref, meta_ref, sink_ref, own_ref, other_ref, q_ref, o_ref, kvs, vts, qs, s_scr, cm_scr
+    inv_ref, meta_ref, sink_ref, k0, k1, k2, k3, o0, o1, o2, o3, q_ref, o_ref, kvs, vts, qs, s_scr, cm_scr
 ):
-    off = meta_ref[0]
+    x_own = meta_ref[0]
     y_tile = meta_ref[1]
     core = meta_ref[2]
+    off = (2 * x_own + core) * ROWS
 
     @pl.loop(0, NBLK)
     def _(s):
         b = inv_ref[s]
-        for px in range(4):
-            for ref, at in ((own_ref, core), (other_ref, 1 - core)):
-                start = pl.multiple_of(s * BLK + (2 * px + at) * ROWS, ROWS)
-                kvs[pl.ds(start, ROWS), :] = ref[lax.rem(b, 4), px, b // 4]
+        for step, pair in enumerate(((k0, o0), (k1, o1), (k2, o2), (k3, o3))):
+            for ref, at in zip(pair, (core, 1 - core)):
+                place = 2 * lax.rem(x_own + step, 4) + at
+                start = pl.multiple_of(s * BLK + place * ROWS, ROWS)
+                kvs[pl.ds(start, ROWS), :] = ref[b]
         t = jnp.transpose(kvs[pl.ds(pl.multiple_of(s * BLK, BLK), BLK), :])
         vts[s, 0:HEAD, :] = t[HEAD : 2 * HEAD, :]
         vts[s, HEAD : HEAD + 16, :] = jnp.ones((16, BLK), BF)
@@ -110,7 +112,7 @@
         attend_kernel,
         out_shape=jax.ShapeDtypeStruct((NBLK, 32, 128), BF),
         in_specs=[pl.BlockSpec(memory_space=pltpu.SMEM)] * 3
-        + [pl.BlockSpec(memory_space=pltpu.VMEM)] * 3,
+        + [pl.BlockSpec(memory_space=pltpu.VMEM)] * 9,
         out_specs=pl.BlockSpec(memory_space=pltpu.VMEM),
         scratch_shapes=[
             pltpu.VMEM((NBLK * BLK, 2 * HEAD), BF),
@@ -121,7 +123,7 @@
         ],
         compiler_params=pltpu.CompilerParams(vmem_limit_bytes=50 * 2**20),
         name="attend",
-    )(inv, meta, sink, own, other, q)
+    )(inv, meta, sink, *own, *other, q)
 
 
 def pull(value, axis, shift):
@@ -167,11 +169,12 @@
     first, second = keys[:, :, 0], keys[:, :, 1]
     keys = jnp.concatenate([first * cos - second * sin, second * cos + first * sin], axis=-1)
     pair = jnp.concatenate([keys, kv[:, 512:].reshape(ROWS, 8, HEAD)], axis=-1).astype(BF)
-    pair = lax.all_to_all(jnp.transpose(pair, (1, 0, 2)), "z", 0, 0, tiled=True)
-    copies = jnp.broadcast_to(pair[None], (16, 8, ROWS, 2 * HEAD)).reshape(128, ROWS, 2 * HEAD)
-    own = lax.all_to_all(copies, ("y", "x"), 0, 0, tiled=True)
-    own = own.reshape(4, 4, 8, ROWS, 2 * HEAD)
-    other = swap(own)
+    pair = jnp.transpose(pair.reshape(ROWS, 4, 2, 2 * HEAD), (2, 1, 0, 3))
+    pair = jnp.broadcast_to(pair[:, None], (2, 4, 4, ROWS, 2 * HEAD)).reshape(32, ROWS, 2 * HEAD)
+    pair = lax.all_to_all(pair, ("z", "y"), 0, 0, tiled=True)
+    own = [pair] + [pull(pair, "x", s) for s in (1, 3, 2)]
+    own[2], own[3] = own[3], own[2]
+    other = [swap(t) for t in own]
 
     rows = jnp.concatenate(row_pieces, axis=0)
     weights = jnp.concatenate(weight_pieces, axis=0)
@@ -186,18 +189,17 @@
 
     q = ordered(project(weights), project(weights_other), c)
     q = lax.dynamic_slice_in_dim(jnp.concatenate([q, q], axis=1), (4 - x) % 4, 4, 1)
-    q = jnp.transpose(q.reshape(2, 2, 2, HEAD, 4 * ROWS), (2, 0, 1, 3, 4))
-    q = lax.all_to_all(q.reshape(8, HEAD, 4 * ROWS), "y", 0, 0, tiled=True)
+    q = jnp.transpose(q, (1, 0, 2, 3)).reshape(8, HEAD, 4 * ROWS)
     q = lax.all_to_all(q, "z", 0, 0, tiled=True)
 
     slot = jnp.arange(3, dtype=jnp.int32)
-    meta = jnp.where(slot == 0, ROWS * (2 * x + c), jnp.where(slot == 1, z // 2, c))
-    sink = lax.dynamic_slice_in_dim(sinks, 4 * z + y, 1, 0)
+    meta = jnp.where(slot == 0, x, jnp.where(slot == 1, y, c))
+    sink = lax.dynamic_slice_in_dim(sinks, 8 * y + z, 1, 0)
     out = attend(block_of, meta.astype(jnp.int32), sink, own, other, q)
 
     out = lax.all_to_all(out, ("z", "y"), 0, 0, tiled=True)
-    out = out.reshape(32, 32, 2, HEAD)
-    return jnp.transpose(out, (2, 1, 0, 3)).reshape(ROWS, 32 * HEAD)
+    out = out.reshape(8, 4, 32, 2, HEAD)
+    return jnp.transpose(out, (3, 2, 1, 0, 4)).reshape(ROWS, 32 * HEAD)
 
 
 def solution(mesh):

time: 177 us -> 153 us (0.86)
  the two profiles are of different devices: /device:TPU:2 before, /device:TPU:1 now
where the time goes in v1:
time: 153 us
  starting transfers between devices  48.1 us (31%)
  Pallas kernels  47.1 us (31%)
  waiting for transfers between devices  17.3 us (11%)
  blocking collectives  15.4 us (10%)
  local copies, waits for them, and re-layouts  11.2 us (7%)
  matrix products  8.55 us (6%)
  other arithmetic  4.51 us (3%)
    pallas_call x1, Pallas kernels, attend(): pl.pallas_call(attend_kernel, out_shape=jax.ShapeDtypeStruct((NBLK, 32, 1...  47.1 us
    ppermute x5, starting transfers between devices, swap(): return lax.ppermute(value, 'c', [(0, 1), (1, 0)])  21.2 us
    all_to_all x1, blocking collectives, per_device(): out = lax.all_to_all(out, ('z', 'y'), 0, 0, tiled=True)  15.4 us
    ppermute x9, starting transfers between devices, pull(): lax.ppermute(value, axis, [((i + shift) % size, i) for i in range(size)])  12.1 us
    all_to_all x1, waiting for transfers between devices, per_device(): q = lax.all_to_all(q, 'z', 0, 0, tiled=True)  11.6 us
    all_to_all x1, starting transfers between devices, per_device(): pair = lax.all_to_all(pair, ('z', 'y'), 0, 0, tiled=True)  10.9 us
    dot_general x2, matrix products, project(): lax.dot_general(w, rows, (((1,), (1,)), ((), ())), preferred_element_type...  4.57 us
    dot_general x1, matrix products, per_device(): kv = jnp.dot(tokens, key_value_weight, preferred_element_type=F32)  3.98 us
  transfers between devices with their start and end apart: 16, of which 3 were waited for; matrix products, arithmetic and copies ran while one was open for 14% of the time, Pallas kernels for 0%

profile of v1, /device:TPU:1, one launch (start us, length us, event | category | flops | bytes accessed | tf_op | source)
XLA Modules:
  0.0 152.7 jit_solution(13194879239809160756)
XLA Ops:
  0.0 3.3 %collective-permute-start.7 = (bf16[64,2880]{1,0:T(8,128)(2,1)}, bf16[64,2880]{1,0:T(8,128)(2,1)S(1)}, u32[]{:S(2)}, u32[]{:S(2)}) collective-permute-start(bf16[64,2880]{1,0:T(8,128)(2,1)} %bitcast.108), channel_id=1, source_target_pairs={{2,0},{4,2},{6,4},{0,6},{3,1},{5,3},{7,5},{1,7},{10,8},{12,10},{14... | collective-permute-start | bytes 1105928 | tf_op jit(solution)/shard_map/ppermute | solution.py:131
  3.3 0.5 collective-permute-start.8
  3.8 0.6 collective-permute-start.9
  4.4 2.7 %collective-permute-start.10 = (bf16[64,2880]{1,0:T(8,128)(2,1)}, bf16[64,2880]{1,0:T(8,128)(2,1)}, u32[]{:S(2)}, u32[]{:S(2)}) collective-permute-start(bf16[64,2880]{1,0:T(8,128)(2,1)} %param.5), channel_id=1, source_target_pairs={{8,0},{16,8},{24,16},{0,24},{9,1},{17,9},{25,17},{1,25},{10,2},{18... | collective-permute-start | bytes 1105928 | tf_op jit(solution)/shard_map/ppermute | solution.py:131
  7.2 0.3 collective-permute-start.11
  7.5 4.0 %fusion.17 = f32[64,1024]{1,0:T(8,128)S(1)} fusion(bf16[64,2880]{1,0:T(8,128)(2,1)} %param.5, bf16[2880,1024]{1,0:T(8,128)(2,1)} %param.7), kind=kOutput, calls=%fused_computation.61 | convolution fusion | flops 377487360 | bytes 6529024 | tf_op jit(solution)/shard_map/dot_general | solution.py:167
  11.6 0.2 select_reduce_fusion.1
  11.8 0.1 fusion.15
  11.9 0.1 copy.69
  12.0 0.1 multiply_cosine_fusion.1
  12.2 0.1 copy.70
  12.4 0.1 copy.71
  12.5 0.1 concatenate.46
  12.6 0.6 maximum_bitcast_fusion
  13.2 0.9 broadcast_in_dim.42
  14.2 10.9 %all-to-all-start = ((bf16[32,64,128]{2,1,0:T(8,128)(2,1)}), bf16[32,64,128]{2,1,0:T(8,128)(2,1)S(1)}, u32[]{:S(2)}, u32[]{:S(2)}) async-start(bf16[32,64,128]{2,1,0:T(8,128)(2,1)} %bitcast.5), calls=%async_computation | async-start | bytes 1048576 | tf_op jit(solution)/shard_map/all_to_all | solution.py:174
  25.1 0.1 convert_element_type.34
  25.2 1.0 constant_dynamic-update-slice_fusion.3
  26.2 1.3 collective-permute-start.12
  27.5 0.8 copy-done.4
  28.3 1.4 pad_maximum_fusion
  29.7 1.6 %copy.76 = bf16[256,2880]{0,1:T(8,128)(2,1)} copy(bf16[256,2880]{1,0:T(8,128)(2,1)S(1)} %pad_maximum_fusion) | data formatting | bytes 2949120 | tf_op jit(solution)/shard_map/concatenate | solution.py:180
  31.4 2.9 %collective-permute-start.13 = (bf16[256,2880]{0,1:T(8,128)(2,1)}, bf16[256,2880]{0,1:T(8,128)(2,1)}, u32[]{:S(2)}, u32[]{:S(2)}) collective-permute-start(bf16[256,2880]{0,1:T(8,128)(2,1)} %copy.76), channel_id=1, source_target_pairs={{0,1},{1,0},{2,3},{3,2},{4,5},{5,4},{6,7},{7,6},{8,9},{9,8},{10,11... | collective-permute-start | bytes 4423688 | tf_op jit(solution)/shard_map/ppermute | solution.py:135
  34.3 0.8 multiply_cosine_fusion
  35.1 1.0 constant_dynamic-update-slice_fusion.2
  36.2 1.0 constant_dynamic-update-slice_fusion.1
  37.2 2.6 %all-to-all-done.k0 = bf16[32,64,128]{2,1,0:T(8,128)(2,1)S(1)} async-done(((bf16[32,64,128]{2,1,0:T(8,128)(2,1)}), bf16[32,64,128]{2,1,0:T(8,128)(2,1)S(1)}, u32[]{:S(2)}, u32[]{:S(2)}) %all-to-all-start) | async-done | bytes 524320 | tf_op jit(solution)/shard_map/all_to_all | solution.py:174
  39.8 2.1 %collective-permute-start = (bf16[32,64,128]{2,1,0:T(8,128)(2,1)S(1)}, bf16[32,64,128]{2,1,0:T(8,128)(2,1)S(1)}, u32[]{:S(2)}, u32[]{:S(2)}) collective-permute-start(bf16[32,64,128]{2,1,0:T(8,128)(2,1)S(1)} %all-to-all-done.k0), channel_id=1, source_target_pairs={{2,0},{4,2},{6,4},{0,6},{3,1},{5,3},{7,5},{1,7},{10,8},{12,10},{14... | collective-permute-start | bytes 1572872 | tf_op jit(solution)/shard_map/ppermute | solution.py:131
  41.8 1.2 collective-permute-start.1
  43.1 1.8 %constant_dynamic-update-slice_fusion = bf16[256,2880]{1,0:T(8,128)(2,1)} fusion(bf16[256,2880]{1,0:T(8,128)(2,1)} %copy-done.1, bf16[64,2880]{1,0:T(8,128)(2,1)} %collective-permute-done.12), kind=kLoop, calls=%fused_computation.42 | loop fusion | bytes 753664 | tf_op jit(solution)/shard_map/concatenate | solution.py:179
  44.9 2.6 %fusion.18 = f32[256,256]{1,0:T(8,128)S(1)} fusion(bf16[256,2880]{1,0:T(8,128)(2,1)} %copy-done, bf16[256,2880]{1,0:T(8,128)(2,1)} %constant_dynamic-update-slice_fusion), kind=kOutput, calls=%fused_computation.62 | convolution fusion | flops 377487360 | bytes 3211264 | tf_op jit(solution)/shard_map/dot_general | solution.py:185
  47.4 4.9 %collective-permute-start.3 = (bf16[32,64,128]{2,1,0:T(8,128)(2,1)S(1)}, bf16[32,64,128]{2,1,0:T(8,128)(2,1)S(1)}, u32[]{:S(2)}, u32[]{:S(2)}) collective-permute-start(bf16[32,64,128]{2,1,0:T(8,128)(2,1)S(1)} %all-to-all-done.k0), channel_id=1, source_target_pairs={{0,1},{1,0},{2,3},{3,2},{4,5},{5,4},{6,7},{7,6},{8,9},{9,8},{10,11... | collective-permute-start | bytes 1572872 | tf_op jit(solution)/shard_map/ppermute | solution.py:135
  52.3 12.9 %collective-permute-start.4 = (bf16[32,64,128]{2,1,0:T(8,128)(2,1)S(1)}, bf16[32,64,128]{2,1,0:T(8,128)(2,1)S(1)}, u32[]{:S(2)}, u32[]{:S(2)}) collective-permute-start(bf16[32,64,128]{2,1,0:T(8,128)(2,1)S(1)} %collective-permute-done.k1), channel_id=1, source_target_pairs={{0,1},{1,0},{2,3},{3,2},{4,5},{5,4},{6,7},{7,6},{8,9},{9,8},{10,11... | collective-permute-start | bytes 1572872 | tf_op jit(solution)/shard_map/ppermute | solution.py:135
  65.2 3.2 %collective-permute-done.2.k3 = bf16[32,64,128]{2,1,0:T(8,128)(2,1)S(1)} collective-permute-done((bf16[32,64,128]{2,1,0:T(8,128)(2,1)S(1)}, bf16[32,64,128]{2,1,0:T(8,128)(2,1)S(1)}, u32[]{:S(2)}, u32[]{:S(2)}) %collective-permute-start.2) | collective-permute-done | bytes 524320 | tf_op jit(solution)/shard_map/ppermute | solution.py:131
  68.4 0.5 collective-permute-start.6
  68.9 2.0 %fusion.19 = f32[256,256]{1,0:T(8,128)S(1)} fusion(bf16[256,2880]{0,1:T(8,128)(2,1)} %collective-permute-done.13, bf16[256,2880]{1,0:T(8,128)(2,1)S(1)} %copy-done.2), kind=kOutput, calls=%fused_computation.63 | convolution fusion | flops 377487360 | bytes 3211264 | tf_op jit(solution)/shard_map/dot_general | solution.py:185
  71.0 0.1 fusion.11
  71.1 0.2 fusion.2
  71.2 0.8 fusion.4
  72.1 3.9 %all-to-all-start.1 = ((bf16[8,64,256]{2,1,0:T(8,128)(2,1)}), bf16[8,64,256]{2,1,0:T(8,128)(2,1)S(1)}, u32[]{:S(2)}, u32[]{:S(2)}) async-start(bf16[8,64,256]{2,1,0:T(8,128)(2,1)} %bitcast.104), calls=%async_computation.1 | async-start | bytes 524288 | tf_op jit(solution)/shard_map/all_to_all | solution.py:193
  75.9 0.6 dynamic_slice.9.sink_ref
  76.6 0.1 select_reduce_fusion.inv_ref
  76.7 11.6 %all-to-all-done.1.q_ref = bf16[8,64,256]{2,1,0:T(8,128)(2,1)S(1)} async-done(((bf16[8,64,256]{2,1,0:T(8,128)(2,1)}), bf16[8,64,256]{2,1,0:T(8,128)(2,1)S(1)}, u32[]{:S(2)}, u32[]{:S(2)}) %all-to-all-start.1) | async-done | bytes 262176 | tf_op jit(solution)/shard_map/all_to_all | solution.py:193
  88.3 47.1 %attend.1 = bf16[32,32,128]{2,1,0:T(8,128)(2,1)S(1)} custom-call(s32[32]{0:T(128)S(1)} %select_reduce_fusion.inv_ref, s32[3]{0:T(128)S(1)} %compare_select_fusion.3.meta_ref, f32[1]{0:T(128)} %dynamic_slice.9.sink_ref, bf16[32,64,128]{2,1,0:T(8,128)(2,1)S(1)} %all-to-all-done.k0, bf16[32,64,128]{2,1,0:T(8,128)(2,1)S(1)} %collective-permute-done.k1, ...), custom_call_target="tpu_custom_call" | custom-call | tf_op jit(solution)/shard_map/attend/pallas_call | solution.py:111
  135.4 15.4 %all_to_all.15 = bf16[32,32,128]{2,1,0:T(8,128)(2,1)S(1)} all-to-all(bf16[32,32,128]{2,1,0:T(8,128)(2,1)S(1)} %attend.1), channel_id=1, replica_groups=mesh['z'=8,'y'=4,'x'=4,'c'=2] {'z','y'}, dimensions={0} | all-to-all | bytes 524288 | tf_op jit(solution)/shard_map/all_to_all | solution.py:200
  150.9 0.2 reshape.277
  151.1 0.3 copy.80
  151.5 1.2 reshape.278
  (43 shorter events, 0.2 us)
Async XLA Ops:
  0.0 26.2 %collective-permute-start.7 = (bf16[64,2880]{1,0:T(8,128)(2,1)}, bf16[64,2880]{1,0:T(8,128)(2,1)S(1)}, u32[]{:S(2)}, u32[]{:S(2)}) collective-permute-start(bf16[64,2880]{1,0:T(8,128)(2,1)} %bitcast.108), channel_id=1, source_target_pairs={{2,0},{4,2},{6,4},{0,6},{3,1},{5,3},{7,5},{1,7},{10,8},{12,10},{14... | collective-permute-start | bytes 1105928 | tf_op jit(solution)/shard_map/ppermute | solution.py:131
  3.3 24.2 %collective-permute-start.8 = (bf16[64,2880]{1,0:T(8,128)(2,1)}, bf16[64,2880]{1,0:T(8,128)(2,1)S(1)}, u32[]{:S(2)}, u32[]{:S(2)}) collective-permute-start(bf16[64,2880]{1,0:T(8,128)(2,1)} %bitcast.109), channel_id=1, source_target_pairs={{4,0},{6,2},{0,4},{2,6},{5,1},{7,3},{1,5},{3,7},{12,8},{14,10},{8,... | collective-permute-start | bytes 1105928 | tf_op jit(solution)/shard_map/ppermute | solution.py:131
  3.8 24.5 %collective-permute-start.9 = (bf16[64,2880]{1,0:T(8,128)(2,1)}, bf16[64,2880]{1,0:T(8,128)(2,1)}, u32[]{:S(2)}, u32[]{:S(2)}) collective-permute-start(bf16[64,2880]{1,0:T(8,128)(2,1)} %bitcast.110), channel_id=1, source_target_pairs={{6,0},{0,2},{2,4},{4,6},{7,1},{1,3},{3,5},{5,7},{14,8},{8,10},{10,... | collective-permute-start | bytes 1105928 | tf_op jit(solution)/shard_map/ppermute | solution.py:131
  4.4 30.7 %collective-permute-start.10 = (bf16[64,2880]{1,0:T(8,128)(2,1)}, bf16[64,2880]{1,0:T(8,128)(2,1)}, u32[]{:S(2)}, u32[]{:S(2)}) collective-permute-start(bf16[64,2880]{1,0:T(8,128)(2,1)} %param.5), channel_id=1, source_target_pairs={{8,0},{16,8},{24,16},{0,24},{9,1},{17,9},{25,17},{1,25},{10,2},{18... | collective-permute-start | bytes 1105928 | tf_op jit(solution)/shard_map/ppermute | solution.py:131
  7.2 29.0 %collective-permute-start.11 = (bf16[64,2880]{1,0:T(8,128)(2,1)}, bf16[64,2880]{1,0:T(8,128)(2,1)}, u32[]{:S(2)}, u32[]{:S(2)}) collective-permute-start(bf16[64,2880]{1,0:T(8,128)(2,1)} %param.5), channel_id=1, source_target_pairs={{16,0},{24,8},{0,16},{8,24},{17,1},{25,9},{1,17},{9,25},{18,2},{26... | collective-permute-start | bytes 1105928 | tf_op jit(solution)/shard_map/ppermute | solution.py:131
  7.5 4.1 %copy-start.8 = (s32[32]{0:T(128)S(1)}, s32[32]{0:T(128)}, u32[]{:S(2)}) copy-start(s32[32]{0:T(128)} %param.8) | copy-start | bytes 388
  14.2 25.6 %all-to-all-start = ((bf16[32,64,128]{2,1,0:T(8,128)(2,1)}), bf16[32,64,128]{2,1,0:T(8,128)(2,1)S(1)}, u32[]{:S(2)}, u32[]{:S(2)}) async-start(bf16[32,64,128]{2,1,0:T(8,128)(2,1)} %bitcast.5), calls=%async_computation | async-start | bytes 1048576 | tf_op jit(solution)/shard_map/all_to_all | solution.py:174
  26.2 1.3 copy-start.3
  26.2 16.9 %collective-permute-start.12 = (bf16[64,2880]{1,0:T(8,128)(2,1)}, bf16[64,2880]{1,0:T(8,128)(2,1)}, u32[]{:S(2)}, u32[]{:S(2)}) collective-permute-start(bf16[64,2880]{1,0:T(8,128)(2,1)} %param.5), channel_id=1, source_target_pairs={{24,0},{0,8},{8,16},{16,24},{25,1},{1,9},{9,17},{17,25},{26,2},{2,... | collective-permute-start | bytes 1105928 | tf_op jit(solution)/shard_map/ppermute | solution.py:131
  27.5 0.8 copy-start.4
  29.7 5.4 %copy-start = (bf16[256,2880]{1,0:T(8,128)(2,1)}, bf16[256,2880]{1,0:T(8,128)(2,1)S(1)}, u32[]{:S(2)}) copy-start(bf16[256,2880]{1,0:T(8,128)(2,1)S(1)} %pad_maximum_fusion) | copy-start | bytes 4423684
  31.4 37.6 %collective-permute-start.13 = (bf16[256,2880]{0,1:T(8,128)(2,1)}, bf16[256,2880]{0,1:T(8,128)(2,1)}, u32[]{:S(2)}, u32[]{:S(2)}) collective-permute-start(bf16[256,2880]{0,1:T(8,128)(2,1)} %copy.76), channel_id=1, source_target_pairs={{0,1},{1,0},{2,3},{3,2},{4,5},{5,4},{6,7},{7,6},{8,9},{9,8},{10,11... | collective-permute-start | bytes 4423688 | tf_op jit(solution)/shard_map/ppermute | solution.py:135
  37.2 4.7 %copy-start.1 = (bf16[256,2880]{1,0:T(8,128)(2,1)}, bf16[256,2880]{1,0:T(8,128)(2,1)S(1)}, u32[]{:S(2)}) copy-start(bf16[256,2880]{1,0:T(8,128)(2,1)S(1)} %constant_dynamic-update-slice_fusion.1) | copy-start | bytes 4423684
  39.8 12.6 %collective-permute-start = (bf16[32,64,128]{2,1,0:T(8,128)(2,1)S(1)}, bf16[32,64,128]{2,1,0:T(8,128)(2,1)S(1)}, u32[]{:S(2)}, u32[]{:S(2)}) collective-permute-start(bf16[32,64,128]{2,1,0:T(8,128)(2,1)S(1)} %all-to-all-done.k0), channel_id=1, source_target_pairs={{2,0},{4,2},{6,4},{0,6},{3,1},{5,3},{7,5},{1,7},{10,8},{12,10},{14... | collective-permute-start | bytes 1572872 | tf_op jit(solution)/shard_map/ppermute | solution.py:131
  41.8 23.4 %collective-permute-start.1 = (bf16[32,64,128]{2,1,0:T(8,128)(2,1)S(1)}, bf16[32,64,128]{2,1,0:T(8,128)(2,1)S(1)}, u32[]{:S(2)}, u32[]{:S(2)}) collective-permute-start(bf16[32,64,128]{2,1,0:T(8,128)(2,1)S(1)} %all-to-all-done.k0), channel_id=1, source_target_pairs={{4,0},{6,2},{0,4},{2,6},{5,1},{7,3},{1,5},{3,7},{12,8},{14,10},{8,... | collective-permute-start | bytes 1572872 | tf_op jit(solution)/shard_map/ppermute | solution.py:131
  43.1 25.3 %collective-permute-start.2 = (bf16[32,64,128]{2,1,0:T(8,128)(2,1)S(1)}, bf16[32,64,128]{2,1,0:T(8,128)(2,1)S(1)}, u32[]{:S(2)}, u32[]{:S(2)}) collective-permute-start(bf16[32,64,128]{2,1,0:T(8,128)(2,1)S(1)} %all-to-all-done.k0), channel_id=1, source_target_pairs={{6,0},{0,2},{2,4},{4,6},{7,1},{1,3},{3,5},{5,7},{14,8},{8,10},{10,... | collective-permute-start | bytes 1572872 | tf_op jit(solution)/shard_map/ppermute | solution.py:131
  44.9 24.1 %copy-start.2 = (bf16[256,2880]{1,0:T(8,128)(2,1)S(1)}, bf16[256,2880]{1,0:T(8,128)(2,1)}, u32[]{:S(2)}) copy-start(bf16[256,2880]{1,0:T(8,128)(2,1)} %constant_dynamic-update-slice_fusion) | copy-start | bytes 4423684
  47.4 23.5 %copy-start.5 = (f32[32,256]{1,0:T(8,128)S(1)}, f32[32,256]{1,0:T(8,128)}, u32[]{:S(2)}) copy-start(f32[32,256]{1,0:T(8,128)} %get-tuple-element.15) | copy-start | bytes 98308
  47.4 23.5 %copy-start.6 = (f32[32,256]{1,0:T(8,128)S(1)}, f32[32,256]{1,0:T(8,128)}, u32[]{:S(2)}) copy-start(f32[32,256]{1,0:T(8,128)} %get-tuple-element.16) | copy-start | bytes 98308
  47.4 29.3 %collective-permute-start.3 = (bf16[32,64,128]{2,1,0:T(8,128)(2,1)S(1)}, bf16[32,64,128]{2,1,0:T(8,128)(2,1)S(1)}, u32[]{:S(2)}, u32[]{:S(2)}) collective-permute-start(bf16[32,64,128]{2,1,0:T(8,128)(2,1)S(1)} %all-to-all-done.k0), channel_id=1, source_target_pairs={{0,1},{1,0},{2,3},{3,2},{4,5},{5,4},{6,7},{7,6},{8,9},{9,8},{10,11... | collective-permute-start | bytes 1572872 | tf_op jit(solution)/shard_map/ppermute | solution.py:135
  52.3 24.4 %collective-permute-start.4 = (bf16[32,64,128]{2,1,0:T(8,128)(2,1)S(1)}, bf16[32,64,128]{2,1,0:T(8,128)(2,1)S(1)}, u32[]{:S(2)}, u32[]{:S(2)}) collective-permute-start(bf16[32,64,128]{2,1,0:T(8,128)(2,1)S(1)} %collective-permute-done.k1), channel_id=1, source_target_pairs={{0,1},{1,0},{2,3},{3,2},{4,5},{5,4},{6,7},{7,6},{8,9},{9,8},{10,11... | collective-permute-start | bytes 1572872 | tf_op jit(solution)/shard_map/ppermute | solution.py:135
  65.2 11.5 %collective-permute-start.5 = (bf16[32,64,128]{2,1,0:T(8,128)(2,1)S(1)}, bf16[32,64,128]{2,1,0:T(8,128)(2,1)}, u32[]{:S(2)}, u32[]{:S(2)}) collective-permute-start(bf16[32,64,128]{2,1,0:T(8,128)(2,1)S(1)} %collective-permute-done.1.k2), channel_id=1, source_target_pairs={{0,1},{1,0},{2,3},{3,2},{4,5},{5,4},{6,7},{7,6},{8,9},{9,8},{10,11... | collective-permute-start | bytes 1572872 | tf_op jit(solution)/shard_map/ppermute | solution.py:135
  68.4 8.3 %collective-permute-start.6 = (bf16[32,64,128]{2,1,0:T(8,128)(2,1)S(1)}, bf16[32,64,128]{2,1,0:T(8,128)(2,1)}, u32[]{:S(2)}, u32[]{:S(2)}) collective-permute-start(bf16[32,64,128]{2,1,0:T(8,128)(2,1)S(1)} %collective-permute-done.2.k3), channel_id=1, source_target_pairs={{0,1},{1,0},{2,3},{3,2},{4,5},{5,4},{6,7},{7,6},{8,9},{9,8},{10,11... | collective-permute-start | bytes 1572872 | tf_op jit(solution)/shard_map/ppermute | solution.py:135
  70.9 5.0 %copy-start.7 = (f32[32]{0:T(128)S(1)}, f32[32]{0:T(128)}, u32[]{:S(2)}) copy-start(f32[32]{0:T(128)} %param.9) | copy-start | bytes 388
  72.1 16.2 %all-to-all-start.1 = ((bf16[8,64,256]{2,1,0:T(8,128)(2,1)}), bf16[8,64,256]{2,1,0:T(8,128)(2,1)S(1)}, u32[]{:S(2)}, u32[]{:S(2)}) async-start(bf16[8,64,256]{2,1,0:T(8,128)(2,1)} %bitcast.104), calls=%async_computation.1 | async-start | bytes 524288 | tf_op jit(solution)/shard_map/all_to_all | solution.py:193

commit v2 on v1

v2 whole, which is shorter than its diff:
```python
import jax
import jax.numpy as jnp
from jax import lax
from jax.experimental import pallas as pl
from jax.experimental.pallas import tpu as pltpu
from jax.sharding import Mesh, PartitionSpec as P


HEAD = 64
NBLK = 32
BLK = 512
ROWS = 64
GROUP = 4 * BLK
ROPE_BASE = 150000.0
NEG = -1e30
EXPC = 1.4426950408889634 / 8.0
BF = jnp.bfloat16
F32 = jnp.float32


def attend_kernel(
    inv_ref, meta_ref, sink_ref, k0, k1, k2, k3, o0, o1, o2, o3, q_ref, o_ref,
    kvs, vts, qs, bias, s_a, s_b, s_c, c_a, c_b, c_c,
):
    x_own = meta_ref[0]
    y_tile = meta_ref[1]
    core = meta_ref[2]
    off = (2 * x_own + core) * ROWS

    def prepare(s, _):
        b = inv_ref[s]
        for step, pair in enumerate(((k0, o0), (k1, o1), (k2, o2), (k3, o3))):
            for ref, at in zip(pair, (core, 1 - core)):
                place = 2 * lax.rem(x_own + step, 4) + at
                start = pl.multiple_of(s * BLK + place * ROWS, ROWS)
                kvs[pl.ds(start, ROWS), :] = ref[b]
        t = jnp.transpose(kvs[pl.ds(pl.multiple_of(s * BLK, BLK), BLK), :])
        vts[s, 0:HEAD, :] = t[HEAD : 2 * HEAD, :]
        vts[s, HEAD : HEAD + 16, :] = jnp.ones((16, BLK), BF)
        return 0

    lax.fori_loop(0, NBLK, prepare, 0, unroll=4)
    for k in range(8):
        rows = jnp.transpose(q_ref[k])
        wide = jnp.concatenate([rows, jnp.zeros((4 * ROWS, HEAD), BF)], axis=1)
        qs[k] = wide.reshape(4, ROWS, 2 * HEAD)

    col = lax.broadcasted_iota(jnp.int32, (1, 256), 1)
    limit = (col // ROWS) * BLK + lax.rem(col, ROWS) + off

    def mask_rows(u, _):
        start = pl.multiple_of(u * 256, 256)
        row = lax.broadcasted_iota(jnp.int32, (256, 256), 0) + start
        bias[pl.ds(start, 256), :] = jnp.where(row <= limit, 0.0, NEG)
        return 0

    lax.fori_loop(0, GROUP // 256, mask_rows, 0)

    def qtile(i):
        parts = []
        for j in range(4):
            b = inv_ref[i * 4 + j]
            parts.append(qs[b // 4, lax.rem(lax.rem(b, 4) - y_tile + 4, 4)])
        return jnp.concatenate(parts, axis=0)

    def qk(q, g, s_ref, c_ref, masked=False):
        top = None
        for u in range(4):
            start = pl.multiple_of(g * GROUP + u * BLK, BLK)
            scores = lax.dot_general(
                kvs[pl.ds(start, BLK), :], q, (((1,), (1,)), ((), ())), preferred_element_type=F32
            )
            if masked:
                scores = scores + bias[u * BLK : (u + 1) * BLK, :]
            s_ref[u * BLK : (u + 1) * BLK, :] = scores
            part = jnp.max(scores.reshape(BLK // 8, 8, 256), axis=0)
            top = part if top is None else jnp.maximum(top, part)
        c_ref[...] = top

    def soft(g, s_ref, c_ref, m, acc, masked=False):
        scores = s_ref[...]
        if masked:
            scores = scores + bias[...]
            top = jnp.max(scores.reshape(GROUP // 8, 8, 256), axis=0)
        else:
            top = c_ref[...]
        new = jnp.maximum(m, jnp.max(top, axis=0, keepdims=True))
        factor = jnp.exp2((m - new) * EXPC)
        weight = jnp.exp2((scores - new) * EXPC).astype(BF)
        values = jnp.concatenate([vts[g * 4 + u] for u in range(4)], axis=1)
        return new, acc * factor + jnp.dot(values, weight, preferred_element_type=F32)

    def finish(i, acc):
        done = jnp.transpose(acc[0:HEAD] / acc[HEAD : HEAD + 1]).astype(BF)
        for j in range(4):
            rows = done[j * ROWS : (j + 1) * ROWS]
            o_ref[inv_ref[i * 4 + j]] = jnp.concatenate([rows[0:32], rows[32:64]], axis=1)

    def two_tiles(i, _):
        a, b = 2 * i, 2 * i + 1
        q_a, q_b, q_next = qtile(a), qtile(b), qtile(jnp.minimum(a + 2, 6))
        m = jnp.full((1, 256), sink_ref[0] * 8.0, F32)
        acc = jnp.concatenate([jnp.zeros((HEAD, 256), F32), jnp.ones((16, 256), F32)], axis=0)

        def full(g, carry):
            m_a, acc_a, m_b, acc_b = carry
            qk(q_b, g, s_b, c_b)
            m_a, acc_a = soft(g, s_a, c_a, m_a, acc_a)
            qk(q_a, g + 1, s_a, c_a)
            m_b, acc_b = soft(g, s_b, c_b, m_b, acc_b)
            return m_a, acc_a, m_b, acc_b

        m_a, acc_a, m_b, acc_b = lax.fori_loop(0, a, full, (m, acc, m, acc))
        qk(q_b, a, s_b, c_b)
        m_a, acc_a = soft(a, s_a, c_a, m_a, acc_a, True)
        qk(q_b, b, s_c, c_c, True)
        m_b, acc_b = soft(a, s_b, c_b, m_b, acc_b)
        finish(a, acc_a)
        qk(q_next, 0, s_a, c_a)
        m_b, acc_b = soft(b, s_c, c_c, m_b, acc_b)
        finish(b, acc_b)
        return 0

    qk(qtile(0), 0, s_a, c_a)
    lax.fori_loop(0, 4, two_tiles, 0)


def attend(inv, meta, sink, own, other, q):
    return pl.pallas_call(
        attend_kernel,
        out_shape=jax.ShapeDtypeStruct((NBLK, 32, 128), BF),
        in_specs=[pl.BlockSpec(memory_space=pltpu.SMEM)] * 3
        + [pl.BlockSpec(memory_space=pltpu.VMEM)] * 9,
        out_specs=pl.BlockSpec(memory_space=pltpu.VMEM),
        scratch_shapes=[
            pltpu.VMEM((NBLK * BLK, 2 * HEAD), BF),
            pltpu.VMEM((NBLK, HEAD + 16, BLK), BF),
            pltpu.VMEM((8, 4, ROWS, 2 * HEAD), BF),
            pltpu.VMEM((GROUP, 256), F32),
        ]
        + [pltpu.VMEM((GROUP, 256), F32)] * 3
        + [pltpu.VMEM((8, 256), F32)] * 3,
        compiler_params=pltpu.CompilerParams(vmem_limit_bytes=50 * 2**20),
        name="attend",
    )(inv, meta, sink, *own, *other, q)


def project_kernel(
    meta_ref, cos_ref, sin_ref, r0, r1, r2, r3, w0, w1, w2, w3, v0, v1, v2, v3, q_ref, rows, weights
):
    x_own = meta_ref[0]
    core = meta_ref[2]
    width = r0.shape[1]
    edge = width // 128 * 128
    rows[:, edge:] = jnp.zeros((rows.shape[0], rows.shape[1] - edge), BF)
    weights[:, edge:] = jnp.zeros((weights.shape[0], weights.shape[1] - edge), BF)
    for s, ref in enumerate((r0, r1, r2, r3)):
        rows[s * ROWS : (s + 1) * ROWS, 0:width] = ref[...]
    for s, ref in enumerate((w0, w1, w2, w3, v0, v1, v2, v3)):
        weights[s * HEAD : (s + 1) * HEAD, 0:width] = ref[...]
    q = lax.dot_general(
        weights[...], rows[...], (((1,), (1,)), ((), ())), preferred_element_type=F32
    )
    cos, sin = cos_ref[...], sin_ref[...]
    for s in range(8):
        a = q[s * HEAD : s * HEAD + 32]
        b = q[s * HEAD + 32 : (s + 1) * HEAD]
        turned = jnp.concatenate([a * cos - b * sin, b * cos + a * sin], axis=0).astype(BF)
        side = core if s < 4 else 1 - core
        q_ref[2 * lax.rem(x_own + s % 4, 4) + side] = turned


def project(meta, cos, sin, rows, weights, others):
    return pl.pallas_call(
        project_kernel,
        out_shape=jax.ShapeDtypeStruct((8, HEAD, 4 * ROWS), BF),
        in_specs=[pl.BlockSpec(memory_space=pltpu.SMEM)]
        + [pl.BlockSpec(memory_space=pltpu.VMEM)] * 14,
        out_specs=pl.BlockSpec(memory_space=pltpu.VMEM),
        scratch_shapes=[pltpu.VMEM((4 * ROWS, 3072), BF), pltpu.VMEM((8 * HEAD, 3072), BF)],
        compiler_params=pltpu.CompilerParams(vmem_limit_bytes=32 * 2**20),
        name="project",
    )(meta, cos, sin, *rows, *weights, *others)


def pull(value, axis, shift):
    size = lax.axis_size(axis)
    return lax.ppermute(value, axis, [((i + shift) % size, i) for i in range(size)])


def swap(value):
    return lax.ppermute(value, "c", [(0, 1), (1, 0)])


def rotations(places):
    inverse = ROPE_BASE ** (-(jnp.arange(HEAD // 2, dtype=F32) * 2.0) / HEAD)
    angles = places.astype(F32)[None, :] * inverse[:, None]
    return jnp.cos(angles), jnp.sin(angles)


def per_device(tokens, query_weight, key_value_weight, block_places, sinks):
    z, y, x, c = (lax.axis_index(a) for a in "zyxc")
    weight_rows = query_weight.T
    row_pieces = [tokens] + [pull(tokens, "y", s) for s in (1, 2, 3)]
    weight_pieces = [weight_rows] + [pull(weight_rows, "x", s) for s in (1, 2, 3)]

    table = jnp.arange(NBLK, dtype=jnp.int32)
    block_of = jnp.sum(
        jnp.where(block_places[None, :] == table[:, None], table[None, :], 0), axis=1
    ).astype(jnp.int32)
    own_blocks = 4 * z + (y + jnp.arange(4, dtype=jnp.int32)) % 4
    own_places = jnp.sum(
        jnp.where(own_blocks[:, None] == table[None, :], block_places[None, :], 0), axis=1
    )
    places = (
        own_places[:, None] * BLK + (2 * x + c) * ROWS + jnp.arange(ROWS, dtype=jnp.int32)[None, :]
    )

    cos, sin = (t.T[:, None, :] for t in rotations(places[0]))
    kv = jnp.dot(tokens, key_value_weight, preferred_element_type=F32)
    keys = kv[:, :512].reshape(ROWS, 8, 2, 32)
    first, second = keys[:, :, 0], keys[:, :, 1]
    keys = jnp.concatenate([first * cos - second * sin, second * cos + first * sin], axis=-1)
    pair = jnp.concatenate([keys, kv[:, 512:].reshape(ROWS, 8, HEAD)], axis=-1).astype(BF)
    pair = jnp.transpose(pair.reshape(ROWS, 4, 2, 2 * HEAD), (2, 1, 0, 3))
    pair = jnp.broadcast_to(pair[:, None], (2, 4, 4, ROWS, 2 * HEAD)).reshape(32, ROWS, 2 * HEAD)
    pair = lax.all_to_all(pair, ("z", "y"), 0, 0, tiled=True)
    own = [pair] + [pull(pair, "x", s) for s in (1, 3, 2)]
    own[2], own[3] = own[3], own[2]
    other = [swap(t) for t in own]

    other_pieces = [swap(t) for t in weight_pieces]
    slot = jnp.arange(3, dtype=jnp.int32)
    meta = jnp.where(slot == 0, x, jnp.where(slot == 1, y, c)).astype(jnp.int32)
    cos_q, sin_q = rotations(places.reshape(4 * ROWS))
    q = project(meta, cos_q, sin_q, row_pieces, weight_pieces, other_pieces)
    q = lax.all_to_all(q, "z", 0, 0, tiled=True)

    sink = lax.dynamic_slice_in_dim(sinks, 8 * y + z, 1, 0)
    out = attend(block_of, meta, sink, own, other, q)

    out = lax.all_to_all(out, ("z", "y"), 0, 0, tiled=True)
    out = out.reshape(8, 4, 32, 2, HEAD)
    return jnp.transpose(out, (3, 2, 1, 0, 4)).reshape(ROWS, 32 * HEAD)


def solution(mesh):
    fine = Mesh(mesh.devices.reshape(8, 4, 4, 2), ("z", "y", "x", "c"))
    whole = ("z", "y", "x", "c")

    return jax.shard_map(
        per_device,
        mesh=fine,
        in_specs=(P(whole, None), P(None, ("y", "x", "c")), P(), P(), P()),
        out_specs=P(whole, None),
        check_vma=False,
    )
```

time: 153 us -> 144 us (0.941)
  waiting for transfers between devices: 17.3 us -> 39.1 us
  Pallas kernels: 47.1 us -> 30.3 us
  starting transfers between devices: 48.1 us -> 38.7 us
  matrix products: 8.55 us -> 4.02 us
  other arithmetic: 4.51 us -> 1.37 us
  local copies, waits for them, and re-layouts: 11.2 us -> 13.5 us
    ppermute x9, waiting for transfers between devices: 3.19 us -> 26.9 us  [pull(): lax.ppermute(value, axis, [((i + shift) % size, i) for i in range(size)])]
    pallas_call x1, Pallas kernels: 47.1 us -> 27 us  [attend(): pl.pallas_call(attend_kernel, out_shape=jax.ShapeDtypeStruct((NBLK, 32, 1...]
    ppermute x5 -> x8, starting transfers between devices: 21.2 us -> 5.18 us  [swap(): return lax.ppermute(value, 'c', [(0, 1), (1, 0)])]
    unnamed x21 -> x30, local copies, waits for them, and re-layouts: 3.87 us -> 9.65 us
    dot_general x2 -> x0, matrix products: 4.57 us -> none  [project(): lax.dot_general(w, rows, (((1,), (1,)), ((), ())), preferred_element_type...]
    concatenate x2 -> x0, local copies, waits for them, and re-layouts: 3.38 us -> none  [the longest x1 1.77 us: per_device(): rows = jnp.concatenate(row_pieces, axis=0)]
    pallas_call x0 -> x1, Pallas kernels: none -> 3.25 us  [project(): pl.pallas_call(project_kernel, out_shape=jax.ShapeDtypeStruct((8, HEAD, 4...]
    all_to_all x1, starting transfers between devices: 3.88 us -> 6.7 us  [per_device(): q = lax.all_to_all(q, 'z', 0, 0, tiled=True)]
  transfers between devices with their start and end apart: 16 -> 19, of which waited for: 3 -> 7; matrix products, arithmetic and copies ran while one was open for 14% -> 1% of each run, Pallas kernels for 0% -> 2%
where the time goes in v2:
time: 144 us; the launch traced here: 143 us
  waiting for transfers between devices  39.1 us (27%)
  starting transfers between devices  38.7 us (27%)
  Pallas kernels  30.3 us (21%)
  blocking collectives  15.7 us (11%)
  local copies, waits for them, and re-layouts  13.5 us (9%)
  matrix products  4.02 us (3%)
    pallas_call x1, Pallas kernels, attend(): pl.pallas_call(attend_kernel, out_shape=jax.ShapeDtypeStruct((NBLK, 32, 1...  27 us
    ppermute x9, waiting for transfers between devices, pull(): lax.ppermute(value, axis, [((i + shift) % size, i) for i in range(size)])  26.9 us
    all_to_all x1, blocking collectives, per_device(): out = lax.all_to_all(out, ('z', 'y'), 0, 0, tiled=True)  15.7 us
    ppermute x9, starting transfers between devices, pull(): lax.ppermute(value, axis, [((i + shift) % size, i) for i in range(size)])  14.8 us
    all_to_all x1, starting transfers between devices, per_device(): pair = lax.all_to_all(pair, ('z', 'y'), 0, 0, tiled=True)  12 us
    all_to_all x1, waiting for transfers between devices, per_device(): q = lax.all_to_all(q, 'z', 0, 0, tiled=True)  11.7 us
    unnamed x30, local copies, waits for them, and re-layouts  9.65 us
    all_to_all x1, starting transfers between devices, per_device(): q = lax.all_to_all(q, 'z', 0, 0, tiled=True)  6.7 us
  transfers between devices with their start and end apart: 19, of which 7 were waited for; matrix products, arithmetic and copies ran while one was open for 1% of the time, Pallas kernels for 2%

profile of v2, /device:TPU:1, one launch (start us, length us, event | category | flops | bytes accessed | tf_op | source)
XLA Modules:
  0.0 143.0 jit_solution(6256218759589247260)
XLA Ops:
  0.0 4.0 %fusion.8 = f32[64,1024]{1,0:T(8,128)S(1)} fusion(bf16[64,2880]{1,0:T(8,128)(2,1)} %r0.1, bf16[2880,1024]{1,0:T(8,128)(2,1)} %param.7), kind=kOutput, calls=%fused_computation.31 | convolution fusion | flops 377487360 | bytes 6529024 | tf_op jit(solution)/shard_map/dot_general | solution.py:220
  4.1 0.2 select_reduce_fusion.1
  4.4 0.1 concatenate.7
  4.7 0.1 multiply_cosine_fusion.1
  5.2 0.6 maximum_bitcast_fusion
  5.8 0.9 broadcast_in_dim.63
  6.7 12.0 %all-to-all-start = ((bf16[32,64,128]{2,1,0:T(8,128)(2,1)}), bf16[32,64,128]{2,1,0:T(8,128)(2,1)S(1)}, u32[]{:S(2)}, u32[]{:S(2)}) async-start(bf16[32,64,128]{2,1,0:T(8,128)(2,1)} %bitcast.5), calls=%async_computation | async-start | bytes 1048576 | tf_op jit(solution)/shard_map/all_to_all | solution.py:227
  18.7 1.0 collective-permute-start.13
  19.8 1.2 collective-permute-start.12
  21.0 2.4 %collective-permute-start.11 = (bf16[64,2880]{1,0:T(8,128)(2,1)S(1)}, bf16[64,2880]{1,0:T(8,128)(2,1)S(1)}, u32[]{:S(2)}, u32[]{:S(2)}) collective-permute-start(bf16[64,2880]{1,0:T(8,128)(2,1)S(1)} %bitcast.34), channel_id=1, source_target_pairs={{4,0},{6,2},{0,4},{2,6},{5,1},{7,3},{1,5},{3,7},{12,8},{14,10},{8,... | collective-permute-start | bytes 1105928 | tf_op jit(solution)/shard_map/ppermute | solution.py:188
  23.4 1.2 collective-permute-start.10
  24.6 3.0 %collective-permute-start.8 = (bf16[64,2880]{1,0:T(8,128)(2,1)S(1)}, bf16[64,2880]{1,0:T(8,128)(2,1)S(1)}, u32[]{:S(2)}, u32[]{:S(2)}) collective-permute-start(bf16[64,2880]{1,0:T(8,128)(2,1)S(1)} %copy-done), channel_id=1, source_target_pairs={{16,0},{24,8},{0,16},{8,24},{17,1},{25,9},{1,17},{9,25},{18,2},{26... | collective-permute-start | bytes 1105928 | tf_op jit(solution)/shard_map/ppermute | solution.py:188
  27.6 0.7 copy-done.3
  28.4 0.9 collective-permute-start.7
  29.2 2.0 %collective-permute-done.12.w3 = bf16[64,2880]{1,0:T(8,128)(2,1)S(1)} collective-permute-done((bf16[64,2880]{1,0:T(8,128)(2,1)S(1)}, bf16[64,2880]{1,0:T(8,128)(2,1)S(1)}, u32[]{:S(2)}, u32[]{:S(2)}) %collective-permute-start.12) | collective-permute-done | bytes 368672 | tf_op jit(solution)/shard_map/ppermute | solution.py:188
  31.2 1.5 %collective-permute-start.9 = (bf16[64,2880]{1,0:T(8,128)(2,1)S(1)}, bf16[64,2880]{1,0:T(8,128)(2,1)}, u32[]{:S(2)}, u32[]{:S(2)}) collective-permute-start(bf16[64,2880]{1,0:T(8,128)(2,1)S(1)} %copy-done), channel_id=1, source_target_pairs={{24,0},{0,8},{8,16},{16,24},{25,1},{1,9},{9,17},{17,25},{26,2},{2,... | collective-permute-start | bytes 1105928 | tf_op jit(solution)/shard_map/ppermute | solution.py:188
  32.7 7.6 %collective-permute-done.11.w2 = bf16[64,2880]{1,0:T(8,128)(2,1)S(1)} collective-permute-done((bf16[64,2880]{1,0:T(8,128)(2,1)S(1)}, bf16[64,2880]{1,0:T(8,128)(2,1)S(1)}, u32[]{:S(2)}, u32[]{:S(2)}) %collective-permute-start.11) | collective-permute-done | bytes 368672 | tf_op jit(solution)/shard_map/ppermute | solution.py:188
  40.3 0.9 collective-permute-start.16
  41.2 0.7 copy-done.5
  42.0 0.7 copy-done.9
  42.8 2.0 %collective-permute-start.1 = (bf16[32,64,128]{2,1,0:T(8,128)(2,1)S(1)}, bf16[32,64,128]{2,1,0:T(8,128)(2,1)S(1)}, u32[]{:S(2)}, u32[]{:S(2)}) collective-permute-start(bf16[32,64,128]{2,1,0:T(8,128)(2,1)S(1)} %all-to-all-done.k0), channel_id=1, source_target_pairs={{4,0},{6,2},{0,4},{2,6},{5,1},{7,3},{1,5},{3,7},{12,8},{14,10},{8,... | collective-permute-start | bytes 1572872 | tf_op jit(solution)/shard_map/ppermute | solution.py:188
  44.8 1.4 collective-permute-done.7.r1
  46.2 0.7 copy-done.11
  46.9 2.6 %collective-permute-start = (bf16[32,64,128]{2,1,0:T(8,128)(2,1)S(1)}, bf16[32,64,128]{2,1,0:T(8,128)(2,1)S(1)}, u32[]{:S(2)}, u32[]{:S(2)}) collective-permute-start(bf16[32,64,128]{2,1,0:T(8,128)(2,1)S(1)} %all-to-all-done.k0), channel_id=1, source_target_pairs={{2,0},{4,2},{6,4},{0,6},{3,1},{5,3},{7,5},{1,7},{10,8},{12,10},{14... | collective-permute-start | bytes 1572872 | tf_op jit(solution)/shard_map/ppermute | solution.py:188
  49.5 0.8 collective-permute-start.15
  50.3 0.7 copy-done.7
  51.1 0.2 multiply_sine_fusion
  51.3 0.4 collective-permute-done.15.v2
  51.8 0.4 collective-permute-start.3
  52.1 15.8 %collective-permute-done.2.k3 = bf16[32,64,128]{2,1,0:T(8,128)(2,1)S(1)} collective-permute-done((bf16[32,64,128]{2,1,0:T(8,128)(2,1)S(1)}, bf16[32,64,128]{2,1,0:T(8,128)(2,1)S(1)}, u32[]{:S(2)}, u32[]{:S(2)}) %collective-permute-start.2) | collective-permute-done | bytes 524320 | tf_op jit(solution)/shard_map/ppermute | solution.py:188
  67.9 0.9 collective-permute-start.6
  68.8 0.2 collective-permute-done.k1
  69.0 1.1 collective-permute-start.4
  70.2 1.0 copy-done.2
  71.1 1.0 copy-done.4
  72.1 1.0 copy-done.6
  73.1 1.0 copy-done.8
  74.1 1.0 copy-done.10
  75.1 1.0 copy-done.12
  76.1 3.3 %project.1 = bf16[8,64,256]{2,1,0:T(8,128)(2,1)} custom-call(s32[3]{0:T(128)S(1)} %compare_select_fusion.3.meta_ref, f32[32,256]{1,0:T(8,128)S(1)} %get-tuple-element.10.cos_ref, f32[32,256]{1,0:T(8,128)S(1)} %get-tuple-element.9.sin_ref, bf16[64,2880]{1,0:T(8,128)(2,1)S(1)} %copy-done, bf16[64,2880]{1,0:T(8,128)(2,1)S(1)} %copy-done.12, ...), custom_call_target="tpu_custom_call" | custom-call | tf_op jit(solution)/shard_map/project/pallas_call | solution.py:174
  79.3 6.7 %all-to-all-start.1 = ((bf16[8,64,256]{2,1,0:T(8,128)(2,1)}), bf16[8,64,256]{2,1,0:T(8,128)(2,1)S(1)}, u32[]{:S(2)}, u32[]{:S(2)}) async-start(bf16[8,64,256]{2,1,0:T(8,128)(2,1)} %project.1), calls=%async_computation.1 | async-start | bytes 524288 | tf_op jit(solution)/shard_map/all_to_all | solution.py:237
  86.1 0.6 dynamic_slice.3.sink_ref
  86.7 11.7 %all-to-all-done.1.q_ref = bf16[8,64,256]{2,1,0:T(8,128)(2,1)S(1)} async-done(((bf16[8,64,256]{2,1,0:T(8,128)(2,1)}), bf16[8,64,256]{2,1,0:T(8,128)(2,1)S(1)}, u32[]{:S(2)}, u32[]{:S(2)}) %all-to-all-start.1) | async-done | bytes 262176 | tf_op jit(solution)/shard_map/all_to_all | solution.py:237
  98.4 27.0 %attend.1 = bf16[32,32,128]{2,1,0:T(8,128)(2,1)S(1)} custom-call(s32[32]{0:T(128)S(1)} %select_reduce_fusion.inv_ref, s32[3]{0:T(128)S(1)} %compare_select_fusion.3.meta_ref, f32[1]{0:T(128)} %dynamic_slice.3.sink_ref, bf16[32,64,128]{2,1,0:T(8,128)(2,1)S(1)} %all-to-all-done.k0, bf16[32,64,128]{2,1,0:T(8,128)(2,1)S(1)} %collective-permute-done.k1, ...), custom_call_target="tpu_custom_call" | custom-call | tf_op jit(solution)/shard_map/attend/pallas_call | solution.py:129
  125.5 15.7 %all_to_all.15 = bf16[32,32,128]{2,1,0:T(8,128)(2,1)S(1)} all-to-all(bf16[32,32,128]{2,1,0:T(8,128)(2,1)S(1)} %attend.1), channel_id=1, replica_groups=mesh['z'=8,'y'=4,'x'=4,'c'=2] {'z','y'}, dimensions={0} | all-to-all | bytes 524288 | tf_op jit(solution)/shard_map/all_to_all | solution.py:242
  141.2 0.2 reshape.124
  141.4 0.3 copy.26
  141.8 1.2 reshape.125
  (50 shorter events, 0.9 us)
Async XLA Ops:
  0.0 24.6 %copy-start = (bf16[64,2880]{1,0:T(8,128)(2,1)S(1)}, bf16[64,2880]{1,0:T(8,128)(2,1)}, u32[]{:S(2)}) copy-start(bf16[64,2880]{1,0:T(8,128)(2,1)} %r0.1) | copy-start | bytes 1105924
  0.0 4.1 %copy-start.14 = (s32[32]{0:T(128)S(1)}, s32[32]{0:T(128)}, u32[]{:S(2)}) copy-start(s32[32]{0:T(128)} %param.8) | copy-start | bytes 388
  0.0 18.7 %copy-start.1 = (bf16[2880,64]{0,1:T(8,128)(2,1)S(1)}, bf16[2880,64]{0,1:T(8,128)(2,1)}, u32[]{:S(2)}) copy-start(bf16[2880,64]{0,1:T(8,128)(2,1)} %param.6) | copy-start | bytes 1105924
  4.1 82.0 %copy-start.13 = (f32[32]{0:T(128)S(1)}, f32[32]{0:T(128)}, u32[]{:S(2)}) copy-start(f32[32]{0:T(128)} %param.9) | copy-start | bytes 388
  6.7 35.3 %all-to-all-start = ((bf16[32,64,128]{2,1,0:T(8,128)(2,1)}), bf16[32,64,128]{2,1,0:T(8,128)(2,1)S(1)}, u32[]{:S(2)}, u32[]{:S(2)}) async-start(bf16[32,64,128]{2,1,0:T(8,128)(2,1)} %bitcast.5), calls=%async_computation | async-start | bytes 1048576 | tf_op jit(solution)/shard_map/all_to_all | solution.py:227
  18.7 8.9 %collective-permute-start.13 = (bf16[64,2880]{1,0:T(8,128)(2,1)S(1)}, bf16[64,2880]{1,0:T(8,128)(2,1)S(1)}, u32[]{:S(2)}, u32[]{:S(2)}) collective-permute-start(bf16[64,2880]{1,0:T(8,128)(2,1)S(1)} %bitcast.32), channel_id=1, source_target_pairs={{0,1},{1,0},{2,3},{3,2},{4,5},{5,4},{6,7},{7,6},{8,9},{9,8},{10,11... | collective-permute-start | bytes 1105928 | tf_op jit(solution)/shard_map/ppermute | solution.py:192
  19.8 11.4 %collective-permute-start.12 = (bf16[64,2880]{1,0:T(8,128)(2,1)S(1)}, bf16[64,2880]{1,0:T(8,128)(2,1)S(1)}, u32[]{:S(2)}, u32[]{:S(2)}) collective-permute-start(bf16[64,2880]{1,0:T(8,128)(2,1)S(1)} %bitcast.33), channel_id=1, source_target_pairs={{6,0},{0,2},{2,4},{4,6},{7,1},{1,3},{3,5},{5,7},{14,8},{8,10},{10,... | collective-permute-start | bytes 1105928 | tf_op jit(solution)/shard_map/ppermute | solution.py:188
  21.0 19.3 %collective-permute-start.11 = (bf16[64,2880]{1,0:T(8,128)(2,1)S(1)}, bf16[64,2880]{1,0:T(8,128)(2,1)S(1)}, u32[]{:S(2)}, u32[]{:S(2)}) collective-permute-start(bf16[64,2880]{1,0:T(8,128)(2,1)S(1)} %bitcast.34), channel_id=1, source_target_pairs={{4,0},{6,2},{0,4},{2,6},{5,1},{7,3},{1,5},{3,7},{12,8},{14,10},{8,... | collective-permute-start | bytes 1105928 | tf_op jit(solution)/shard_map/ppermute | solution.py:188
  23.4 18.5 %collective-permute-start.10 = (bf16[64,2880]{1,0:T(8,128)(2,1)S(1)}, bf16[64,2880]{1,0:T(8,128)(2,1)}, u32[]{:S(2)}, u32[]{:S(2)}) collective-permute-start(bf16[64,2880]{1,0:T(8,128)(2,1)S(1)} %bitcast.35), channel_id=1, source_target_pairs={{2,0},{4,2},{6,4},{0,6},{3,1},{5,3},{7,5},{1,7},{10,8},{12,10},{14... | collective-permute-start | bytes 1105928 | tf_op jit(solution)/shard_map/ppermute | solution.py:188
  24.6 17.4 %collective-permute-start.8 = (bf16[64,2880]{1,0:T(8,128)(2,1)S(1)}, bf16[64,2880]{1,0:T(8,128)(2,1)S(1)}, u32[]{:S(2)}, u32[]{:S(2)}) collective-permute-start(bf16[64,2880]{1,0:T(8,128)(2,1)S(1)} %copy-done), channel_id=1, source_target_pairs={{16,0},{24,8},{0,16},{8,24},{17,1},{25,9},{1,17},{9,25},{18,2},{26... | collective-permute-start | bytes 1105928 | tf_op jit(solution)/shard_map/ppermute | solution.py:188
  27.6 0.7 copy-start.3
  28.4 17.8 %collective-permute-start.7 = (bf16[64,2880]{1,0:T(8,128)(2,1)S(1)}, bf16[64,2880]{1,0:T(8,128)(2,1)S(1)}, u32[]{:S(2)}, u32[]{:S(2)}) collective-permute-start(bf16[64,2880]{1,0:T(8,128)(2,1)S(1)} %copy-done), channel_id=1, source_target_pairs={{8,0},{16,8},{24,16},{0,24},{9,1},{17,9},{25,17},{1,25},{10,2},{18... | collective-permute-start | bytes 1105928 | tf_op jit(solution)/shard_map/ppermute | solution.py:188
  31.2 18.3 %collective-permute-start.9 = (bf16[64,2880]{1,0:T(8,128)(2,1)S(1)}, bf16[64,2880]{1,0:T(8,128)(2,1)}, u32[]{:S(2)}, u32[]{:S(2)}) collective-permute-start(bf16[64,2880]{1,0:T(8,128)(2,1)S(1)} %copy-done), channel_id=1, source_target_pairs={{24,0},{0,8},{8,16},{16,24},{25,1},{1,9},{9,17},{17,25},{26,2},{2,... | collective-permute-start | bytes 1105928 | tf_op jit(solution)/shard_map/ppermute | solution.py:188
  40.3 10.8 %collective-permute-start.16 = (bf16[64,2880]{1,0:T(8,128)(2,1)S(1)}, bf16[64,2880]{1,0:T(8,128)(2,1)}, u32[]{:S(2)}, u32[]{:S(2)}) collective-permute-start(bf16[64,2880]{1,0:T(8,128)(2,1)S(1)} %collective-permute-done.12.w3), channel_id=1, source_target_pairs={{0,1},{1,0},{2,3},{3,2},{4,5},{5,4},{6,7},{7,6},{8,9},{9,8},{10,11... | collective-permute-start | bytes 1105928 | tf_op jit(solution)/shard_map/ppermute | solution.py:192
  41.2 0.7 copy-start.5
  42.0 25.9 %collective-permute-start.2 = (bf16[32,64,128]{2,1,0:T(8,128)(2,1)S(1)}, bf16[32,64,128]{2,1,0:T(8,128)(2,1)S(1)}, u32[]{:S(2)}, u32[]{:S(2)}) collective-permute-start(bf16[32,64,128]{2,1,0:T(8,128)(2,1)S(1)} %all-to-all-done.k0), channel_id=1, source_target_pairs={{6,0},{0,2},{2,4},{4,6},{7,1},{1,3},{3,5},{5,7},{14,8},{8,10},{10,... | collective-permute-start | bytes 1572872 | tf_op jit(solution)/shard_map/ppermute | solution.py:188
  42.0 0.7 copy-start.9
  42.8 26.0 %collective-permute-start.1 = (bf16[32,64,128]{2,1,0:T(8,128)(2,1)S(1)}, bf16[32,64,128]{2,1,0:T(8,128)(2,1)S(1)}, u32[]{:S(2)}, u32[]{:S(2)}) collective-permute-start(bf16[32,64,128]{2,1,0:T(8,128)(2,1)S(1)} %all-to-all-done.k0), channel_id=1, source_target_pairs={{4,0},{6,2},{0,4},{2,6},{5,1},{7,3},{1,5},{3,7},{12,8},{14,10},{8,... | collective-permute-start | bytes 1572872 | tf_op jit(solution)/shard_map/ppermute | solution.py:188
  46.2 0.7 copy-start.11
  46.9 22.1 %collective-permute-start = (bf16[32,64,128]{2,1,0:T(8,128)(2,1)S(1)}, bf16[32,64,128]{2,1,0:T(8,128)(2,1)S(1)}, u32[]{:S(2)}, u32[]{:S(2)}) collective-permute-start(bf16[32,64,128]{2,1,0:T(8,128)(2,1)S(1)} %all-to-all-done.k0), channel_id=1, source_target_pairs={{2,0},{4,2},{6,4},{0,6},{3,1},{5,3},{7,5},{1,7},{10,8},{12,10},{14... | collective-permute-start | bytes 1572872 | tf_op jit(solution)/shard_map/ppermute | solution.py:188
  49.5 2.3 %collective-permute-start.15 = (bf16[64,2880]{1,0:T(8,128)(2,1)S(1)}, bf16[64,2880]{1,0:T(8,128)(2,1)}, u32[]{:S(2)}, u32[]{:S(2)}) collective-permute-start(bf16[64,2880]{1,0:T(8,128)(2,1)S(1)} %collective-permute-done.11.w2), channel_id=1, source_target_pairs={{0,1},{1,0},{2,3},{3,2},{4,5},{5,4},{6,7},{7,6},{8,9},{9,8},{10,11... | collective-permute-start | bytes 1105928 | tf_op jit(solution)/shard_map/ppermute | solution.py:192
  50.3 0.7 copy-start.7
  51.0 19.1 %collective-permute-start.14 = (bf16[64,2880]{1,0:T(8,128)(2,1)}, bf16[64,2880]{1,0:T(8,128)(2,1)}, u32[]{:S(2)}, u32[]{:S(2)}) collective-permute-start(bf16[64,2880]{1,0:T(8,128)(2,1)} %collective-permute-done.10.w1), channel_id=1, source_target_pairs={{0,1},{1,0},{2,3},{3,2},{4,5},{5,4},{6,7},{7,6},{8,9},{9,8},{10,11... | collective-permute-start | bytes 1105928 | tf_op jit(solution)/shard_map/ppermute | solution.py:192
  51.8 46.7 %collective-permute-start.3 = (bf16[32,64,128]{2,1,0:T(8,128)(2,1)S(1)}, bf16[32,64,128]{2,1,0:T(8,128)(2,1)S(1)}, u32[]{:S(2)}, u32[]{:S(2)}) collective-permute-start(bf16[32,64,128]{2,1,0:T(8,128)(2,1)S(1)} %all-to-all-done.k0), channel_id=1, source_target_pairs={{0,1},{1,0},{2,3},{3,2},{4,5},{5,4},{6,7},{7,6},{8,9},{9,8},{10,11... | collective-permute-start | bytes 1572872 | tf_op jit(solution)/shard_map/ppermute | solution.py:192
  67.9 30.5 %collective-permute-start.6 = (bf16[32,64,128]{2,1,0:T(8,128)(2,1)S(1)}, bf16[32,64,128]{2,1,0:T(8,128)(2,1)}, u32[]{:S(2)}, u32[]{:S(2)}) collective-permute-start(bf16[32,64,128]{2,1,0:T(8,128)(2,1)S(1)} %collective-permute-done.2.k3), channel_id=1, source_target_pairs={{0,1},{1,0},{2,3},{3,2},{4,5},{5,4},{6,7},{7,6},{8,9},{9,8},{10,11... | collective-permute-start | bytes 1572872 | tf_op jit(solution)/shard_map/ppermute | solution.py:192
  68.8 29.7 %collective-permute-start.5 = (bf16[32,64,128]{2,1,0:T(8,128)(2,1)S(1)}, bf16[32,64,128]{2,1,0:T(8,128)(2,1)}, u32[]{:S(2)}, u32[]{:S(2)}) collective-permute-start(bf16[32,64,128]{2,1,0:T(8,128)(2,1)S(1)} %collective-permute-done.1.k2), channel_id=1, source_target_pairs={{0,1},{1,0},{2,3},{3,2},{4,5},{5,4},{6,7},{7,6},{8,9},{9,8},{10,11... | collective-permute-start | bytes 1572872 | tf_op jit(solution)/shard_map/ppermute | solution.py:192
  69.0 29.4 %collective-permute-start.4 = (bf16[32,64,128]{2,1,0:T(8,128)(2,1)S(1)}, bf16[32,64,128]{2,1,0:T(8,128)(2,1)S(1)}, u32[]{:S(2)}, u32[]{:S(2)}) collective-permute-start(bf16[32,64,128]{2,1,0:T(8,128)(2,1)S(1)} %collective-permute-done.k1), channel_id=1, source_target_pairs={{0,1},{1,0},{2,3},{3,2},{4,5},{5,4},{6,7},{7,6},{8,9},{9,8},{10,11... | collective-permute-start | bytes 1572872 | tf_op jit(solution)/shard_map/ppermute | solution.py:192
  70.2 1.0 copy-start.2
  71.1 1.0 copy-start.4
  72.1 1.0 copy-start.6
  73.1 1.0 copy-start.8
  74.1 1.0 copy-start.10
  75.1 1.0 copy-start.12
  79.3 19.1 %all-to-all-start.1 = ((bf16[8,64,256]{2,1,0:T(8,128)(2,1)}), bf16[8,64,256]{2,1,0:T(8,128)(2,1)S(1)}, u32[]{:S(2)}, u32[]{:S(2)}) async-start(bf16[8,64,256]{2,1,0:T(8,128)(2,1)} %project.1), calls=%async_computation.1 | async-start | bytes 524288 | tf_op jit(solution)/shard_map/all_to_all | solution.py:237
